TPU v7x, 128 devices: a whole 4x4x4 slice. The times are simulated.
128 devices in a mesh: band: 32 (over x, y, core), grid: 4 (over z).
Axes of the slice: x: 4, y: 4, z: 4, core: 2. Of those that a mesh axis runs over, the one named last changes fastest.
Arguments:
- orbitals: bfloat16 [256, 128, 128, 128], P('band', None, 'grid'), may hold values from -0.375 to 0.375
- occupations: float32 [256], P('band'), may hold values from 0 to 2
- rho_in: float32 [128, 128, 128], P('band', 'grid'), may hold values from 0.5 to 1.5
- hist_in: float32 [7, 128, 128, 128], P(None, 'band', 'grid'), may hold values from 0.5 to 1.5
- hist_res: float32 [7, 128, 128, 128], P(None, 'band', 'grid'), may hold values from -10 to 10
Outputs:
- rho_next: float32 [128, 128, 128], P('band', 'grid')
- v_hartree: float32 [128, 128, 128], P('band', 'grid')
All inputs are finite; a program needn't handle non-finite values.
Results may differ from a plain program's by a relative error of at most 0.0003.
Values sent between devices are 32-bit elements; how exact they have to be, the bound alone decides.
A program may use at most 64 MiB of HBM per device.

v0:
```python
import jax
import jax.numpy as jnp
from jax import lax
from jax.sharding import Mesh
from jax.sharding import PartitionSpec as P

BAND = ("band_0", "band_1", "band_2")
BAND_GRID = ("band_0", "band_1", "band_2", "grid")


beta_mix = 0.5
spacing = 0.2
highest = lax.Precision.HIGHEST
einsum_forms = {1: "jk,mkbc->mjbc", 2: "jk,makc->majc", 3: "jk,mabk->mabj"}


def cut_along(shard, dim, length):
    dims = shard.shape
    blocks = shard.reshape(*dims[:dim], length, dims[dim] // length, *dims[dim + 1 :])
    return jnp.moveaxis(blocks, dim, 0)


def summed_on_arrival(shard, axis, dim):
    length = lax.axis_size(axis)
    blocks = lax.all_to_all(cut_along(shard, dim, length), axis, 0, 0, tiled=True)
    return jnp.sum(blocks, axis=0)


def by_axis(shard, axes):
    for axis in axes:
        shard = lax.psum(shard, axis)
    return shard


def dft_tables(length):
    positions = jnp.arange(length, dtype=jnp.int32)
    phases = positions[:, None] * positions[None, :] % length
    angles = phases.astype(jnp.float32) * (2.0 * jnp.pi / length)
    return (jnp.cos(angles), jnp.sin(angles))


def transform(real_part, imag_part, axis_dim, inverse):
    length = real_part.shape[axis_dim]
    cosine_table, sine_table = dft_tables(length)
    layout_form = einsum_forms[axis_dim]
    cos_real = jnp.einsum(layout_form, cosine_table, real_part, precision=highest)
    sin_real = jnp.einsum(layout_form, sine_table, real_part, precision=highest)
    cos_imag = jnp.einsum(layout_form, cosine_table, imag_part, precision=highest)
    sin_imag = jnp.einsum(layout_form, sine_table, imag_part, precision=highest)
    if inverse:
        return ((cos_real - sin_imag) / length, (cos_imag + sin_real) / length)
    return (cos_real + sin_imag, cos_imag - sin_real)


def transform_real(real_part, imag_part, axis_dim):
    length = real_part.shape[axis_dim]
    cosine_table, sine_table = dft_tables(length)
    layout_form = einsum_forms[axis_dim]
    cos_real = jnp.einsum(layout_form, cosine_table, real_part, precision=highest)
    sin_imag = jnp.einsum(layout_form, sine_table, imag_part, precision=highest)
    return (cos_real - sin_imag) / length


def forward(density):
    zero_imag = jnp.zeros_like(density)
    real_part, imag_part = transform(density, zero_imag, 3, False)
    complex_pair = (
        lax.all_to_all(real_part, BAND, split_axis=3, concat_axis=1, tiled=True),
        lax.all_to_all(imag_part, BAND, split_axis=3, concat_axis=1, tiled=True),
    )
    real_part, imag_part = transform(complex_pair[0], complex_pair[1], 1, False)
    complex_pair = (
        lax.all_to_all(real_part, "grid", split_axis=1, concat_axis=2, tiled=True),
        lax.all_to_all(imag_part, "grid", split_axis=1, concat_axis=2, tiled=True),
    )
    return transform(complex_pair[0], complex_pair[1], 2, False)


def inverse_real(real_part, imag_part):
    real_part, imag_part = transform(real_part, imag_part, 2, True)
    complex_pair = (
        lax.all_to_all(real_part, "grid", split_axis=2, concat_axis=1, tiled=True),
        lax.all_to_all(imag_part, "grid", split_axis=2, concat_axis=1, tiled=True),
    )
    real_part, imag_part = transform(complex_pair[0], complex_pair[1], 1, True)
    complex_pair = (
        lax.all_to_all(real_part, BAND, split_axis=1, concat_axis=3, tiled=True),
        lax.all_to_all(imag_part, BAND, split_axis=1, concat_axis=3, tiled=True),
    )
    return transform_real(complex_pair[0], complex_pair[1], 3)


def kernel_block(rows_first, rows_last, length):

    def frequency(amount, offset):
        positions = offset + jnp.arange(amount, dtype=jnp.int32)
        return jnp.where(positions < length // 2, positions, positions - length)

    freq_first = frequency(rows_first, lax.axis_index("grid") * rows_first)
    freq_middle = frequency(length, 0)
    freq_last = frequency(rows_last, lax.axis_index(BAND) * rows_last)
    squared_sum = (
        (freq_first * freq_first)[:, None, None]
        + (freq_middle * freq_middle)[None, :, None]
        + (freq_last * freq_last)[None, None, :]
    )
    cell_len = length * spacing
    floored = jnp.maximum(squared_sum, 1).astype(jnp.float32)
    values_all = cell_len * cell_len / jnp.pi / floored
    return jnp.where(squared_sum > 0, values_all, jnp.zeros_like(values_all))[None]


def pulay_weights(gram_matrix):
    factor = jnp.linalg.cholesky(gram_matrix)
    solved = jax.scipy.linalg.cho_solve(
        (factor, True), jnp.ones((gram_matrix.shape[0],), jnp.float32)
    )
    return solved / jnp.sum(solved)


def local(orbitals, occupations, rho_in, hist_in, hist_res):
    grid_len = rho_in.shape[2]
    orbital_rows = orbitals.astype(jnp.float32)
    rho_out = summed_on_arrival(
        jnp.sum(occupations[:, None, None, None] * orbital_rows * orbital_rows, axis=0), BAND, 0
    )
    res_new = rho_out - rho_in
    residuals = jnp.concatenate([hist_res, res_new[None]], axis=0)
    inputs = jnp.concatenate([hist_in, rho_in[None]], axis=0)
    vectors = residuals.shape[0]
    flat_res = residuals.reshape(vectors, -1)
    gram_part = jnp.dot(flat_res, flat_res.T, precision=highest, preferred_element_type=jnp.float32)
    trials = inputs + beta_mix * residuals
    gram_matrix = by_axis(gram_part, BAND_GRID) / (grid_len * grid_len * grid_len)
    weights = pulay_weights(gram_matrix)
    rho_next = jnp.tensordot(weights, trials, axes=1, precision=highest)
    spec_real, spec_imag = forward(rho_next[None])
    kernel = kernel_block(spec_real.shape[1], spec_real.shape[3], grid_len)
    potential = inverse_real(spec_real * kernel, spec_imag * kernel)
    return (rho_next, potential[0])


def solution(mesh):
    finer = Mesh(
        mesh.devices.reshape(4, 4, 2, mesh.shape["grid"]), ("band_0", "band_1", "band_2", "grid")
    )
    in_specs = (
        P(BAND, None, "grid", None),
        P(BAND),
        P(BAND, "grid", None),
        P(None, BAND, "grid", None),
        P(None, BAND, "grid", None),
    )
    out_specs = (P(BAND, "grid", None), P(BAND, "grid", None))
    return jax.shard_map(local, mesh=finer, in_specs=in_specs, out_specs=out_specs, check_vma=False)
```

profile of v0, /device:TPU:1, one launch (start us, length us, event | category | flops | bytes accessed | tf_op | source)
XLA Modules:
  0.0 181.9 jit_solution(7918294195818698000)
XLA Ops:
  0.7 7.3 %fusion = f32[128,32,128]{2,1,0:T(8,128)} fusion(bf16[8,128,32,128]{3,2,1,0:T(8,128)(2,1)} %param.5, f32[8]{0:T(128)} %param.6), kind=kLoop, calls=%fused_computation.1 | loop fusion | flops 16252928 | bytes 10485792 | tf_op jit(solution)/shard_map/reduce_sum | solution.py:125
  7.9 8.6 %all-to-all-start = ((f32[32,4,32,128]{3,2,1,0:T(8,128)}), f32[32,4,32,128]{3,2,1,0:T(8,128)S(1)}, u32[]{:S(2)}, u32[]{:S(2)}) async-start(f32[32,4,32,128]{3,2,1,0:T(8,128)} %bitcast.204), calls=%async_computation | async-start | bytes 4194304 | tf_op jit(solution)/shard_map/all_to_all | solution.py:25
  16.8 1.3 copy.78
  18.7 26.1 %all-to-all-done = f32[32,4,32,128]{3,2,1,0:T(8,128)S(1)} async-done(((f32[32,4,32,128]{3,2,1,0:T(8,128)}), f32[32,4,32,128]{3,2,1,0:T(8,128)S(1)}, u32[]{:S(2)}, u32[]{:S(2)}) %all-to-all-start) | async-done | bytes 2097184 | tf_op jit(solution)/shard_map/all_to_all | solution.py:25
  45.0 1.2 convolution_bitcast_fusion
  46.2 6.6 %psum.28 = f32[8,8]{0,1:T(8,128)S(1)} all-reduce(f32[8,8]{0,1:T(8,128)S(1)} %convolution_bitcast_fusion), channel_id=1, replica_groups=mesh['band_0'=4,'band_1'=4,'band_2'=2,'grid'=4] {'band_0'}, use_global_device_ids=true, to_apply=%region_2.0 | all-reduce | flops 64 | bytes 512 | tf_op jit(solution)/shard_map/psum | solution.py:31
  52.8 6.8 %psum.29 = f32[8,8]{0,1:T(8,128)S(1)} all-reduce(f32[8,8]{0,1:T(8,128)S(1)} %psum.28), channel_id=1, replica_groups=mesh['band_0'=4,'band_1'=4,'band_2'=2,'grid'=4] {'band_1'}, use_global_device_ids=true, to_apply=%region_3.0 | all-reduce | flops 64 | bytes 512 | tf_op jit(solution)/shard_map/psum | solution.py:31
  59.6 7.0 %psum.30 = f32[8,8]{0,1:T(8,128)S(1)} all-reduce(f32[8,8]{0,1:T(8,128)S(1)} %psum.29), channel_id=1, replica_groups=mesh['band_0'=4,'band_1'=4,'band_2'=2,'grid'=4] {'band_2'}, use_global_device_ids=true, to_apply=%region_4.0 | all-reduce | flops 64 | bytes 512 | tf_op jit(solution)/shard_map/psum | solution.py:31
  66.7 9.7 %psum.31 = f32[8,8]{0,1:T(8,128)S(1)} all-reduce(f32[8,8]{0,1:T(8,128)S(1)} %psum.30), channel_id=1, replica_groups=mesh['band_0'=4,'band_1'=4,'band_2'=2,'grid'=4] {'grid'}, use_global_device_ids=true, to_apply=%region_5.0 | all-reduce | flops 64 | bytes 512 | tf_op jit(solution)/shard_map/psum | solution.py:31
  76.5 0.7 cholesky.16
  77.2 0.6 compare_reduce_fusion
  77.9 0.6 fusion.88
  79.3 0.8 fusion.192
  80.3 1.2 fusion.95
  82.7 0.8 reshape.228
  83.5 5.9 %all-to-all-start.2 = ((f32[32,1,512]{2,1,0:T(1,128)}), f32[32,1,512]{2,1,0:T(1,128)S(1)}, u32[]{:S(2)}, u32[]{:S(2)}) async-start(f32[32,1,512]{2,1,0:T(1,128)} %reshape.228), calls=%async_computation.2 | async-start | bytes 131072 | tf_op jit(solution)/shard_map/all_to_all | solution.py:69
  90.0 0.8 reshape.226
  90.9 6.0 %all-to-all-done.2 = f32[32,1,512]{2,1,0:T(1,128)S(1)} async-done(((f32[32,1,512]{2,1,0:T(1,128)}), f32[32,1,512]{2,1,0:T(1,128)S(1)}, u32[]{:S(2)}, u32[]{:S(2)}) %all-to-all-start.2) | async-done | bytes 65568 | tf_op jit(solution)/shard_map/all_to_all | solution.py:69
  96.8 3.9 %all-to-all-start.1 = ((f32[32,1,512]{2,1,0:T(1,128)}), f32[32,1,512]{2,1,0:T(1,128)S(1)}, u32[]{:S(2)}, u32[]{:S(2)}) async-start(f32[32,1,512]{2,1,0:T(1,128)} %reshape.226), calls=%async_computation.1 | async-start | bytes 131072 | tf_op jit(solution)/shard_map/all_to_all | solution.py:68
  101.3 0.8 reduce.7
  103.1 5.1 %all-to-all-done.1 = f32[32,1,512]{2,1,0:T(1,128)S(1)} async-done(((f32[32,1,512]{2,1,0:T(1,128)}), f32[32,1,512]{2,1,0:T(1,128)S(1)}, u32[]{:S(2)}, u32[]{:S(2)}) %all-to-all-start.1) | async-done | bytes 65568 | tf_op jit(solution)/shard_map/all_to_all | solution.py:68
  108.2 0.8 reduce.6
  110.0 0.6 fusion.14
  110.8 0.8 reshape.232
  111.6 3.3 %all-to-all-start.4 = ((f32[4,1,4096]{2,1,0:T(1,128)}), f32[4,1,4096]{2,1,0:T(1,128)S(1)}, u32[]{:S(2)}, u32[]{:S(2)}) async-start(f32[4,1,4096]{2,1,0:T(1,128)} %reshape.232), calls=%async_computation.4 | async-start | bytes 131072 | tf_op jit(solution)/shard_map/all_to_all | solution.py:74
  115.7 0.8 reshape.230
  116.6 2.8 %all-to-all-done.4 = f32[4,1,4096]{2,1,0:T(1,128)S(1)} async-done(((f32[4,1,4096]{2,1,0:T(1,128)}), f32[4,1,4096]{2,1,0:T(1,128)S(1)}, u32[]{:S(2)}, u32[]{:S(2)}) %all-to-all-start.4) | async-done | bytes 65568 | tf_op jit(solution)/shard_map/all_to_all | solution.py:74
  119.4 3.3 %all-to-all-start.3 = ((f32[4,1,4096]{2,1,0:T(1,128)}), f32[4,1,4096]{2,1,0:T(1,128)S(1)}, u32[]{:S(2)}, u32[]{:S(2)}) async-start(f32[4,1,4096]{2,1,0:T(1,128)} %reshape.230), calls=%async_computation.3 | async-start | bytes 131072 | tf_op jit(solution)/shard_map/all_to_all | solution.py:73
  122.7 0.8 reduce.9
  124.5 2.6 %all-to-all-done.3 = f32[4,1,4096]{2,1,0:T(1,128)S(1)} async-done(((f32[4,1,4096]{2,1,0:T(1,128)}), f32[4,1,4096]{2,1,0:T(1,128)S(1)}, u32[]{:S(2)}, u32[]{:S(2)}) %all-to-all-start.3) | async-done | bytes 65568 | tf_op jit(solution)/shard_map/all_to_all | solution.py:73
  127.1 0.8 reduce.8
  131.6 0.8 reshape.236
  132.4 3.3 %all-to-all-start.6 = ((f32[4,1,4096]{2,1,0:T(1,128)}), f32[4,1,4096]{2,1,0:T(1,128)S(1)}, u32[]{:S(2)}, u32[]{:S(2)}) async-start(f32[4,1,4096]{2,1,0:T(1,128)} %reshape.236), calls=%async_computation.6 | async-start | bytes 131072 | tf_op jit(solution)/shard_map/all_to_all | solution.py:83
  136.4 0.8 reshape.234
  137.2 2.9 %all-to-all-done.6 = f32[4,1,4096]{2,1,0:T(1,128)S(1)} async-done(((f32[4,1,4096]{2,1,0:T(1,128)}), f32[4,1,4096]{2,1,0:T(1,128)S(1)}, u32[]{:S(2)}, u32[]{:S(2)}) %all-to-all-start.6) | async-done | bytes 65568 | tf_op jit(solution)/shard_map/all_to_all | solution.py:83
  140.2 3.3 %all-to-all-start.5 = ((f32[4,1,4096]{2,1,0:T(1,128)}), f32[4,1,4096]{2,1,0:T(1,128)S(1)}, u32[]{:S(2)}, u32[]{:S(2)}) async-start(f32[4,1,4096]{2,1,0:T(1,128)} %reshape.234), calls=%async_computation.5 | async-start | bytes 131072 | tf_op jit(solution)/shard_map/all_to_all | solution.py:82
  143.5 0.8 reduce.11
  145.3 2.6 %all-to-all-done.5 = f32[4,1,4096]{2,1,0:T(1,128)S(1)} async-done(((f32[4,1,4096]{2,1,0:T(1,128)}), f32[4,1,4096]{2,1,0:T(1,128)S(1)}, u32[]{:S(2)}, u32[]{:S(2)}) %all-to-all-start.5) | async-done | bytes 65568 | tf_op jit(solution)/shard_map/all_to_all | solution.py:82
  147.9 0.8 reduce.10
  150.4 0.8 reshape.240
  151.2 8.7 %all-to-all-start.8 = ((f32[32,1,512]{2,1,0:T(1,128)}), f32[32,1,512]{2,1,0:T(1,128)S(1)}, u32[]{:S(2)}, u32[]{:S(2)}) async-start(f32[32,1,512]{2,1,0:T(1,128)} %reshape.240), calls=%async_computation.8 | async-start | bytes 131072 | tf_op jit(solution)/shard_map/all_to_all | solution.py:88
  160.6 0.8 reshape.238
  161.4 6.0 %all-to-all-done.8 = f32[32,1,512]{2,1,0:T(1,128)S(1)} async-done(((f32[32,1,512]{2,1,0:T(1,128)}), f32[32,1,512]{2,1,0:T(1,128)S(1)}, u32[]{:S(2)}, u32[]{:S(2)}) %all-to-all-start.8) | async-done | bytes 65568 | tf_op jit(solution)/shard_map/all_to_all | solution.py:88
  167.4 3.9 %all-to-all-start.7 = ((f32[32,1,512]{2,1,0:T(1,128)}), f32[32,1,512]{2,1,0:T(1,128)S(1)}, u32[]{:S(2)}, u32[]{:S(2)}) async-start(f32[32,1,512]{2,1,0:T(1,128)} %reshape.238), calls=%async_computation.7 | async-start | bytes 131072 | tf_op jit(solution)/shard_map/all_to_all | solution.py:87
  171.3 0.8 reduce.13
  172.5 6.3 %all-to-all-done.7 = f32[32,1,512]{2,1,0:T(1,128)S(1)} async-done(((f32[32,1,512]{2,1,0:T(1,128)}), f32[32,1,512]{2,1,0:T(1,128)S(1)}, u32[]{:S(2)}, u32[]{:S(2)}) %all-to-all-start.7) | async-done | bytes 65568 | tf_op jit(solution)/shard_map/all_to_all | solution.py:87
  178.8 0.8 reduce.12
  180.6 1.3 fusion.13
  (73 shorter events, 17.6 us)
Async XLA Ops:
  0.6 15.9 %copy-start = (f32[7,4,32,128]{3,2,1,0:T(8,128)S(1)}, f32[7,4,32,128]{3,2,1,0:T(8,128)}, u32[]{:S(2)}) copy-start(f32[7,4,32,128]{3,2,1,0:T(8,128)} %param.9) | copy-start | bytes 1376260
  0.6 44.4 %copy-start.1 = (f32[4,32,128]{2,1,0:T(8,128)S(1)}, f32[4,32,128]{2,1,0:T(8,128)}, u32[]{:S(2)}) copy-start(f32[4,32,128]{2,1,0:T(8,128)} %param.7) | copy-start | bytes 196612
  7.9 36.9 %all-to-all-start = ((f32[32,4,32,128]{3,2,1,0:T(8,128)}), f32[32,4,32,128]{3,2,1,0:T(8,128)S(1)}, u32[]{:S(2)}, u32[]{:S(2)}) async-start(f32[32,4,32,128]{3,2,1,0:T(8,128)} %bitcast.204), calls=%async_computation | async-start | bytes 4194304 | tf_op jit(solution)/shard_map/all_to_all | solution.py:25
  81.5 63.3 %copy-start.2 = (f32[1,16384]{1,0:T(1,128)}, f32[1,16384]{1,0:T(1,128)S(1)}, u32[]{:S(2)}) copy-start(f32[1,16384]{1,0:T(1,128)S(1)} %fusion.95) | copy-start | bytes 196612
  83.5 13.3 %all-to-all-start.2 = ((f32[32,1,512]{2,1,0:T(1,128)}), f32[32,1,512]{2,1,0:T(1,128)S(1)}, u32[]{:S(2)}, u32[]{:S(2)}) async-start(f32[32,1,512]{2,1,0:T(1,128)} %reshape.228), calls=%async_computation.2 | async-start | bytes 131072 | tf_op jit(solution)/shard_map/all_to_all | solution.py:69
  96.8 11.4 %all-to-all-start.1 = ((f32[32,1,512]{2,1,0:T(1,128)}), f32[32,1,512]{2,1,0:T(1,128)S(1)}, u32[]{:S(2)}, u32[]{:S(2)}) async-start(f32[32,1,512]{2,1,0:T(1,128)} %reshape.226), calls=%async_computation.1 | async-start | bytes 131072 | tf_op jit(solution)/shard_map/all_to_all | solution.py:68
  111.6 7.7 %all-to-all-start.4 = ((f32[4,1,4096]{2,1,0:T(1,128)}), f32[4,1,4096]{2,1,0:T(1,128)S(1)}, u32[]{:S(2)}, u32[]{:S(2)}) async-start(f32[4,1,4096]{2,1,0:T(1,128)} %reshape.232), calls=%async_computation.4 | async-start | bytes 131072 | tf_op jit(solution)/shard_map/all_to_all | solution.py:74
  119.4 7.7 %all-to-all-start.3 = ((f32[4,1,4096]{2,1,0:T(1,128)}), f32[4,1,4096]{2,1,0:T(1,128)S(1)}, u32[]{:S(2)}, u32[]{:S(2)}) async-start(f32[4,1,4096]{2,1,0:T(1,128)} %reshape.230), calls=%async_computation.3 | async-start | bytes 131072 | tf_op jit(solution)/shard_map/all_to_all | solution.py:73
  132.4 7.7 %all-to-all-start.6 = ((f32[4,1,4096]{2,1,0:T(1,128)}), f32[4,1,4096]{2,1,0:T(1,128)S(1)}, u32[]{:S(2)}, u32[]{:S(2)}) async-start(f32[4,1,4096]{2,1,0:T(1,128)} %reshape.236), calls=%async_computation.6 | async-start | bytes 131072 | tf_op jit(solution)/shard_map/all_to_all | solution.py:83
  140.2 7.7 %all-to-all-start.5 = ((f32[4,1,4096]{2,1,0:T(1,128)}), f32[4,1,4096]{2,1,0:T(1,128)S(1)}, u32[]{:S(2)}, u32[]{:S(2)}) async-start(f32[4,1,4096]{2,1,0:T(1,128)} %reshape.234), calls=%async_computation.5 | async-start | bytes 131072 | tf_op jit(solution)/shard_map/all_to_all | solution.py:82
  151.2 16.2 %all-to-all-start.8 = ((f32[32,1,512]{2,1,0:T(1,128)}), f32[32,1,512]{2,1,0:T(1,128)S(1)}, u32[]{:S(2)}, u32[]{:S(2)}) async-start(f32[32,1,512]{2,1,0:T(1,128)} %reshape.240), calls=%async_computation.8 | async-start | bytes 131072 | tf_op jit(solution)/shard_map/all_to_all | solution.py:88
  167.4 11.4 %all-to-all-start.7 = ((f32[32,1,512]{2,1,0:T(1,128)}), f32[32,1,512]{2,1,0:T(1,128)S(1)}, u32[]{:S(2)}, u32[]{:S(2)}) async-start(f32[32,1,512]{2,1,0:T(1,128)} %reshape.238), calls=%async_computation.7 | async-start | bytes 131072 | tf_op jit(solution)/shard_map/all_to_all | solution.py:87
where the time goes:
time: 183 us; the launch traced here: 182 us
  waiting for transfers between devices  60.5 us (33%)
  starting transfers between devices  44.1 us (24%)
  blocking collectives  30.2 us (17%)
  other arithmetic  16.6 us (9%)
  matrix products  15.8 us (9%)
  local copies, waits for them, and re-layouts  13.6 us (7%)
    psum x4, blocking collectives, by_axis(): shard = lax.psum(shard, axis)  30.2 us
    all_to_all x1, waiting for transfers between devices, summed_on_arrival(): lax.all_to_all(cut_along(shard, dim, length), axis, 0, 0, tiled=True)  26.1 us
    unnamed x24, local copies, waits for them, and re-layouts  9.62 us
    all_to_all x1, starting transfers between devices, inverse_real(): lax.all_to_all(imag_part, BAND, split_axis=1, concat_axis=3, tiled=True)  8.71 us
    all_to_all x1, starting transfers between devices, summed_on_arrival(): lax.all_to_all(cut_along(shard, dim, length), axis, 0, 0, tiled=True)  8.58 us
    reduce_sum x1, other arithmetic, local(): jnp.sum(occupations[:, None, None, None] * orbital_rows * orbital_rows, a...  7.28 us
    all_to_all x1, waiting for transfers between devices, inverse_real(): lax.all_to_all(real_part, BAND, split_axis=1, concat_axis=3, tiled=True)  6.32 us
    all_to_all x1, waiting for transfers between devices, forward(): lax.all_to_all(imag_part, BAND, split_axis=3, concat_axis=1, tiled=True)  5.98 us
  transfers between devices with their start and end apart: 9, of which 9 were waited for; matrix products, arithmetic and copies ran while one was open for 8% of the time, Pallas kernels for 0%

commit v1 on v0

v1 whole, which is shorter than its diff:
```python
import functools

import jax
import jax.numpy as jnp
import numpy as np
from jax import lax
from jax.experimental import pallas as pl
from jax.experimental.pallas import tpu as pltpu
from jax.sharding import Mesh
from jax.sharding import PartitionSpec as P

LOGICAL = pl.DeviceIdType.LOGICAL
BAND = ("x", "y", "c")
N = 128
HIST = 7
CHUNKS = 16
beta_mix = 0.5
spacing = 0.2
f32 = jnp.float32
bf16 = jnp.bfloat16


def tables():
    k = np.arange(N)
    angle = 2.0 * np.pi * ((k[:, None] * k[None, :]) % N) / N
    basis = (np.cos(angle) + np.sin(angle)) / np.sqrt(N)
    order = (4 * np.arange(32)[None, :] + np.arange(4)[:, None]).reshape(-1)
    parts = []
    for table in (basis, basis[:, order], basis[order, :]):
        high = table.astype(jnp.bfloat16)
        low = (table - high.astype(np.float64)).astype(jnp.bfloat16)
        parts += [high, low]
    return jnp.asarray(np.stack(parts))


def halves(value):
    high = value.astype(bf16)
    return high, (value - high.astype(f32)).astype(bf16)


def product(left, right, dims):
    dot = functools.partial(
        lax.dot_general, dimension_numbers=(dims, ((), ())), preferred_element_type=f32
    )
    return dot(left[0], right[0]) + (dot(left[0], right[1]) + dot(left[1], right[0]))


def partner_ids(x, y, c, z):
    plane = {(i, j): ((x + i) % 4) * 32 + ((y + j) % 4) * 8 for i in range(4) for j in range(4)}
    rest = {(i, j): ((c + i) % 2) * 4 + (z + j) % 4 for i in range(2) for j in range(4)}
    slot_plane = {(i, j): ((x + i) % 4) * 8 + ((y + j) % 4) * 2 for i in range(4) for j in range(4)}
    slot_rest = {(i, j): ((c + i) % 2) + ((z + j) % 4) * 32 for i in range(2) for j in range(4)}
    moves = [(a, b, d, e) for a in range(4) for b in range(4) for d in range(2) for e in range(4)][1:]

    def hops(m):
        return sum((0, 1, 2, 1)[m[i]] for i in (0, 1, 3))

    moves.sort(key=lambda m: -hops(m))
    return [
        (plane[m[:2]] + rest[m[2:]], slot_plane[m[:2]] + slot_rest[m[2:]], m) for m in moves
    ]


def kernel(
    orb, occ, rin_h, hin_h, hres_h, tab_h, rho_h, v_h,
    orb_v, rin, hin, hres, tab, part, crecv, r1, r2, r3, r4,
    wide, grow, grecv, xsend, xrecv, vsend, vrecv, rho_v, v_v,
    load_sem, in_sem, out_sem, c_send, c_recv, rs_send, rs_recv, a_send, a_recv,
):
    x, y, c, z = (lax.axis_index(a) for a in ("x", "y", "c", "z"))

    def place(px, py, pc, pz):
        return px * 32 + py * 8 + pc * 4 + pz

    me = place(x, y, c, z)
    band = x * 8 + y * 2 + c
    my_slot = z * 32 + band
    others = partner_ids(x, y, c, z)

    barrier = pltpu.get_barrier_semaphore()
    near = [t for t, _, m in others if sum(v > 0 for v in m) == 1]
    for t in near:
        pl.semaphore_signal(barrier, inc=1, device_id=t, device_id_type=LOGICAL)

    def load(chunk):
        rows = pl.ds(chunk * 8, 8)
        return pltpu.make_async_copy(orb.at[:, rows], orb_v.at[:, rows], load_sem.at[chunk])

    for chunk in range(CHUNKS):
        load(chunk).start()
    inputs = [(tab_h, tab), (rin_h, rin), (hres_h, hres), (hin_h, hin)]
    for i, (a, b) in enumerate(inputs):
        pltpu.make_async_copy(a, b, in_sem.at[i]).start()

    weights_occ = [occ[k] for k in range(8)]

    @pl.loop(0, CHUNKS)
    def _(chunk):
        load(chunk).wait()
        for row in range(8):
            total = None
            for k in range(8):
                value = orb_v[k, chunk * 8 + row].astype(f32)
                term = weights_occ[k] * (value * value)
                total = term if total is None else total + term
            part[chunk // 4, chunk % 4, row // 4, row % 4] = total

    pl.semaphore_wait(barrier, len(near))

    def c_copy(s):
        return pltpu.make_async_remote_copy(
            src_ref=part.at[:, :, 1 - c, s], dst_ref=crecv.at[:, :, s],
            send_sem=c_send.at[s], recv_sem=c_recv.at[s],
            device_id=place(x, y, 1 - c, z), device_id_type=LOGICAL,
        )

    for s in (0, 2, 1, 3):
        c_copy(s).start()

    flip = {
        "x": {1: x + 1 - 2 * (x % 2), 2: (x + 2) % 4, 3: 3 - x},
        "y": {1: y + 1 - 2 * (y % 2), 2: (y + 2) % 4, 3: 3 - y},
    }
    mine = {"x": x, "y": y}
    orders = {0: ("x", "y", 1), 1: ("x", "y", 3), 2: ("y", "x", 1), 3: ("y", "x", 3)}

    def dev(axis, e):
        if axis == "x":
            return place(flip["x"][e], y, c, z)
        return place(x, flip["y"][e], c, z)

    def rows_of(axis, index, s):
        if axis == "x":
            return part.at[index, :, c, s]
        return part.at[:, index, c, s]

    def block_of(axis, index, s):
        if axis == "x":
            return part.at[index, y, c, s]
        return part.at[x, index, c, s]

    def steps(s):
        first, second, e1 = orders[s]
        e2 = 4 - e1
        slot = s * 6

        def remote(src, dst, sem, to):
            return pltpu.make_async_remote_copy(
                src_ref=src, dst_ref=dst, send_sem=rs_send.at[slot + sem],
                recv_sem=rs_recv.at[slot + sem], device_id=to, device_id_type=LOGICAL,
            )

        one = [
            (remote(rows_of(first, flip[first][e1], s), r1.at[s, 0], 0, dev(first, e1)),
             rows_of(first, mine[first], s), r1.at[s, 0]),
            (remote(rows_of(first, flip[first][2], s), r1.at[s, 1], 1, dev(first, e1)),
             rows_of(first, flip[first][e2], s), r1.at[s, 1]),
        ]
        two = [
            (remote(rows_of(first, flip[first][e2], s), r2.at[s], 2, dev(first, e2)),
             rows_of(first, mine[first], s), r2.at[s]),
        ]
        three = [
            (remote(block_of(second, flip[second][e1], s), r3.at[s, 0], 3, dev(second, e1)),
             block_of(second, mine[second], s), r3.at[s, 0]),
            (remote(block_of(second, flip[second][2], s), r3.at[s, 1], 4, dev(second, e1)),
             block_of(second, flip[second][e2], s), r3.at[s, 1]),
        ]
        four = [
            (remote(block_of(second, flip[second][e2], s), r4.at[s], 5, dev(second, e2)),
             block_of(second, mine[second], s), r4.at[s]),
        ]
        return [one, two, three, four]

    plan = {s: steps(s) for s in range(4)}
    for s in (0, 2, 1, 3):
        c_copy(s).wait_recv()
        own = part.at[:, :, c, s]
        own[...] = own[...] + crecv[:, :, s]
        for copy, _, _ in plan[s][0]:
            copy.start()

    for i, (a, b) in enumerate(inputs):
        pltpu.make_async_copy(a, b, in_sem.at[i]).wait()

    lane = lax.broadcasted_iota(jnp.int32, (8, N), 1)
    sub = lax.broadcasted_iota(jnp.int32, (8, N), 0)

    def fold(value):
        return jnp.sum(value.reshape(16, 8, N), axis=0)

    def products(i, field, amount):
        rows = jnp.zeros((8, N), f32)
        for j in range(amount):
            line = jnp.sum(fold(field * hres[j]), axis=0, keepdims=True)
            rows = jnp.where(sub == j, line, rows)
        return rows

    def placed(i, rows):
        total = jnp.sum(rows, axis=1, keepdims=True)
        spots = (lane == 8 * i + sub) | (lane == 8 * sub + i)
        return jnp.sum(jnp.where(spots & (sub <= i), total, 0.0), axis=0, keepdims=True)

    row = jnp.zeros((1, N), f32)
    for i in range(HIST):
        row = row + placed(i, products(i, hres[i], i + 1))

    wide[...] = jnp.zeros_like(wide)
    for half in range(2):
        for g in range(4):
            for a in range(4):
                wide[half, pl.ds(g * 128 + a * 32, 32), pl.ds(a * 128, 128)] = tab[
                    half, pl.ds(g * 32, 32), :
                ]

    for step in range(4):
        for s in (0, 2, 1, 3):
            for copy, into, came in plan[s][step]:
                copy.wait_recv()
                into[...] = into[...] + came[...]
            if step < 3:
                for copy, _, _ in plan[s][step + 1]:
                    copy.start()

    rho_out = part.at[x, y, c]
    new = rho_out[...].reshape(N, N) - rin[...]
    rows = products(7, new, HIST)
    line = jnp.sum(fold(new * new), axis=0, keepdims=True)
    rows = jnp.where(sub == 7, line, rows)
    row = row + placed(7, rows)
    grow[...] = row

    def exchange(source, target, sem):
        copies = []
        for t, slot, _ in others:
            copies.append(pltpu.make_async_remote_copy(
                src_ref=source(t, slot), dst_ref=target,
                send_sem=a_send.at[sem], recv_sem=a_recv.at[sem],
                device_id=t, device_id_type=LOGICAL,
            ))
        for copy in copies:
            copy.start()

    def arrived(buffer, sem):
        pltpu.make_async_copy(buffer.at[pl.ds(0, 127)], buffer.at[pl.ds(0, 127)], a_recv.at[sem]).wait()

    def sent(buffer, sem):
        pltpu.make_async_copy(buffer.at[pl.ds(0, 127)], buffer.at[pl.ds(0, 127)], a_send.at[sem]).wait()

    exchange(lambda t, slot: grow, grecv.at[pl.ds(me, 1)], 0)
    grecv[pl.ds(me, 1)] = row
    arrived(grecv, 0)
    flat = jnp.sum(grecv[...], axis=0, keepdims=True) * (1.0 / (N * N * N))
    matrix = jnp.zeros((8, N), f32)
    for i in range(8):
        shifted = flat if i == 0 else pltpu.roll(flat, N - 8 * i, 1)
        matrix = jnp.where(sub == i, shifted, matrix)
    matrix = jnp.where(lane < 8, matrix, jnp.where(lane == 8, 1.0, 0.0))
    for k in range(8):
        pivot_row = matrix[k : k + 1, :]
        column = jnp.sum(jnp.where(lane == k, matrix, 0.0), axis=1, keepdims=True)
        pivot = column[k : k + 1, :]
        matrix = jnp.where(sub == k, matrix, matrix - (column / pivot) * pivot_row)
    diagonal = jnp.sum(jnp.where(lane == sub, matrix, 0.0), axis=1, keepdims=True)
    right = jnp.sum(jnp.where(lane == 8, matrix, 0.0), axis=1, keepdims=True)
    solved = right / diagonal
    weights = solved / jnp.sum(solved, axis=0, keepdims=True)

    rho = weights[7:8, :] * (rin[...] + beta_mix * new)
    for m in range(HIST):
        rho = rho + weights[m : m + 1, :] * (hin[m] + beta_mix * hres[m])
    rho_v[...] = rho
    out_rho = pltpu.make_async_copy(rho_v, rho_h, out_sem.at[0])
    out_rho.start()

    basis = (tab[0], tab[1])
    xsend[...] = product(basis, halves(rho), ((1,), (1,)))
    xrecv[pl.ds(my_slot, 1)] = xsend[pl.ds(me, 1)]
    exchange(lambda t, slot: xsend.at[pl.ds(t, 1)], xrecv.at[pl.ds(my_slot, 1)], 1)

    freq = jnp.minimum(
        lax.broadcasted_iota(jnp.int32, (N, N), 0), N - lax.broadcasted_iota(jnp.int32, (N, N), 0)
    )
    freq_q = jnp.minimum(
        lax.broadcasted_iota(jnp.int32, (N, N), 1), N - lax.broadcasted_iota(jnp.int32, (N, N), 1)
    )
    freq_r = jnp.minimum(me, N - me)
    squared = freq * freq + freq_q * freq_q + freq_r * freq_r
    cell = N * spacing
    floored = jnp.maximum(squared, 1).astype(f32)
    coulomb = jnp.where(squared > 0, cell * cell / np.pi / floored, 0.0)

    arrived(xrecv, 1)
    joined = jnp.concatenate([xrecv[pl.ds(g * 32, 32)] for g in range(4)], axis=1)
    both = (wide[0], wide[1])
    second = product(halves(joined), both, ((1,), (0,)))
    stacked = jnp.concatenate([second[:, a * 128 : (a + 1) * 128] for a in range(4)], axis=0)
    spectrum = product((tab[2], tab[3]), halves(stacked), ((1,), (0,))) * coulomb
    back = product((tab[4], tab[5]), halves(spectrum), ((1,), (0,)))
    joined = jnp.concatenate([back[a * 32 : (a + 1) * 32] for a in range(4)], axis=1)
    planes = product(halves(joined), both, ((1,), (1,)))
    for g in range(4):
        vsend[pl.ds(g * 32, 32)] = planes[:, g * 128 : (g + 1) * 128]
    vrecv[pl.ds(me, 1)] = vsend[pl.ds(my_slot, 1)]
    exchange(lambda t, slot: vsend.at[pl.ds(slot, 1)], vrecv.at[pl.ds(me, 1)], 2)
    arrived(vrecv, 2)
    v_v[...] = product(halves(vrecv[...].T), basis, ((1,), (0,)))
    out_v = pltpu.make_async_copy(v_v, v_h, out_sem.at[1])
    out_v.start()

    for s in range(4):
        c_copy(s).wait_send()
        for step in plan[s]:
            for copy, _, _ in step:
                copy.wait_send()
    sent(grecv, 0)
    sent(xsend, 1)
    sent(vsend, 2)
    out_rho.wait()
    out_v.wait()


def local(orbitals, occupations, rho_in, hist_in, hist_res):
    anywhere = pl.BlockSpec(memory_space=pl.ANY)
    vmem, dma = pltpu.VMEM, pltpu.SemaphoreType.DMA
    square = (N, N)
    rho, v = pl.pallas_call(
        kernel,
        out_shape=[jax.ShapeDtypeStruct(square, f32)] * 2,
        in_specs=[anywhere, pl.BlockSpec(memory_space=pltpu.SMEM)] + [anywhere] * 4,
        out_specs=[anywhere] * 2,
        scratch_shapes=[
            vmem((8, N, 32, N), bf16), vmem(square, f32), vmem((HIST, N, N), f32),
            vmem((HIST, N, N), f32), vmem((6, N, N), bf16),
            vmem((4, 4, 2, 4, 32, N), f32), vmem((4, 4, 4, 32, N), f32),
            vmem((4, 2, 4, 32, N), f32), vmem((4, 4, 32, N), f32),
            vmem((4, 2, 32, N), f32), vmem((4, 32, N), f32),
            vmem((2, 512, 512), bf16), vmem((1, N), f32), vmem(square, f32),
            vmem(square, f32), vmem(square, f32), vmem(square, f32), vmem(square, f32),
            vmem(square, f32), vmem(square, f32),
            dma((CHUNKS,)), dma((4,)), dma((2,)), dma((4,)), dma((4,)),
            dma((24,)), dma((24,)), dma((3,)), dma((3,)),
        ],
        compiler_params=pltpu.CompilerParams(
            collective_id=0, has_side_effects=True, vmem_limit_bytes=40 * 2**20
        ),
    )(
        orbitals, occupations, rho_in.reshape(square), hist_in.reshape(HIST, N, N),
        hist_res.reshape(HIST, N, N), tables(),
    )
    return rho.reshape(rho_in.shape), v.reshape(rho_in.shape)


def solution(mesh):
    finer = Mesh(mesh.devices.reshape(4, 4, 2, 4), ("x", "y", "c", "z"))
    in_specs = (
        P(BAND, None, "z", None), P(BAND), P(BAND, "z", None),
        P(None, BAND, "z", None), P(None, BAND, "z", None),
    )
    out_specs = (P(BAND, "z", None), P(BAND, "z", None))
    return jax.shard_map(local, mesh=finer, in_specs=in_specs, out_specs=out_specs, check_vma=False)
```

time: 183 us -> 59.7 us (0.33)
  waiting for transfers between devices: 60.5 us -> 0 us
  Pallas kernels: 0 us -> 49.6 us
  starting transfers between devices: 44.1 us -> 0 us
  blocking collectives: 30.2 us -> 0 us
  other arithmetic: 16.6 us -> 0 us
  matrix products: 15.8 us -> 0 us
  local copies, waits for them, and re-layouts: 13.6 us -> 9.09 us
    all_to_all x9 -> x0, waiting for transfers between devices: 60.5 us -> none  [the longest x1 26.1 us: summed_on_arrival(): lax.all_to_all(cut_along(shard, dim, length), axis, 0, 0, tiled=True)]
    pallas_call x0 -> x1, Pallas kernels: none -> 49.6 us  [local(): pl.pallas_call(kernel, out_shape=[jax.ShapeDtypeStruct(square, f32)] * 2,...]
    all_to_all x9 -> x0, starting transfers between devices: 44.1 us -> none  [the longest x1 8.71 us: inverse_real(): lax.all_to_all(imag_part, BAND, split_axis=1, concat_axis=3, tiled=True)]
    psum x4 -> x0, blocking collectives: 30.2 us -> none  [by_axis(): shard = lax.psum(shard, axis)]
    dot_general x23 -> x0, matrix products: 13.8 us -> none  [the longest x5 2.69 us: transform(): sin_real = jnp.einsum(layout_form, sine_table, real_part, precision=highest)]
    reduce_sum x2 -> x0, other arithmetic: 7.42 us -> none  [the longest x1 7.28 us: local(): jnp.sum(occupations[:, None, None, None] * orbital_rows * orbital_rows, a...]
    all_to_all x8 -> x0, other arithmetic: 6.14 us -> none  [the longest x1 0.77 us: forward(): lax.all_to_all(imag_part, 'grid', split_axis=1, concat_axis=2, tiled=True)]
    another operation x5 -> x0, other arithmetic: 2.67 us -> none  [the longest x3 1.39 us: pulay_weights(): factor = jnp.linalg.cholesky(gram_matrix)]
  transfers between devices with their start and end apart: 9 -> 0, of which waited for: 9 -> 0; matrix products, arithmetic and copies ran while one was open for 8% -> 0% of each run, Pallas kernels for 0% -> 0%
where the time goes in v1:
time: 59.7 us; the launch traced here: 59.3 us
  Pallas kernels  49.6 us (83%)
  local copies, waits for them, and re-layouts  9.09 us (15%)
  between operations  0.65 us (1%)
    pallas_call x1, Pallas kernels, local(): pl.pallas_call(kernel, out_shape=[jax.ShapeDtypeStruct(square, f32)] * 2,...  49.6 us
    unnamed x14, local copies, waits for them, and re-layouts  9.09 us

profile of v1, /device:TPU:1, one launch (start us, length us, event | category | flops | bytes accessed | tf_op | source)
XLA Modules:
  0.0 59.3 jit_solution(5114341809251236895)
XLA Ops:
  0.6 0.0 copy-start
  0.6 3.4 %copy-done = bf16[8,128,32,128]{3,2,1,0:T(8,128)(2,1)S(1)} copy-done((bf16[8,128,32,128]{3,2,1,0:T(8,128)(2,1)S(1)}, bf16[8,128,32,128]{3,2,1,0:T(8,128)(2,1)}, u32[]{:S(2)}) %copy-start) | copy-done | bytes 8388632
  4.0 0.0 copy-start.1
  4.0 1.0 %copy-done.1 = f32[7,4,32,128]{3,2,1,0:T(8,128)S(1)} copy-done((f32[7,4,32,128]{3,2,1,0:T(8,128)S(1)}, f32[7,4,32,128]{3,2,1,0:T(8,128)}, u32[]{:S(2)}) %copy-start.1) | copy-done | bytes 458776
  5.0 0.0 copy-start.2
  5.0 1.0 %copy-done.2 = f32[7,4,32,128]{3,2,1,0:T(8,128)S(1)} copy-done((f32[7,4,32,128]{3,2,1,0:T(8,128)S(1)}, f32[7,4,32,128]{3,2,1,0:T(8,128)}, u32[]{:S(2)}) %copy-start.2) | copy-done | bytes 458776
  6.1 0.0 copy-start.3
  6.1 0.9 %copy-done.3 = bf16[6,128,128]{2,1,0:T(8,128)(2,1)S(1)} copy-done((bf16[6,128,128]{2,1,0:T(8,128)(2,1)S(1)}, bf16[6,128,128]{2,1,0:T(8,128)(2,1)}, u32[]{:S(2)}) %copy-start.3) | copy-done | bytes 196632
  7.0 0.0 copy-start.4
  7.0 0.8 %copy-done.4 = f32[4,32,128]{2,1,0:T(8,128)S(1)} copy-done((f32[4,32,128]{2,1,0:T(8,128)S(1)}, f32[4,32,128]{2,1,0:T(8,128)}, u32[]{:S(2)}) %copy-start.4) | copy-done | bytes 65560
  7.8 0.0 copy-start.5
  7.8 0.7 %copy-done.5 = f32[8]{0:T(128)S(1)} copy-done((f32[8]{0:T(128)S(1)}, f32[8]{0:T(128)}, u32[]{:S(2)}) %copy-start.5) | copy-done | bytes 56
  8.5 49.6 %shard_map.77 = (f32[128,128]{1,0:T(8,128)S(1)}, f32[128,128]{1,0:T(8,128)S(1)}) custom-call(bf16[8,128,32,128]{3,2,1,0:T(8,128)(2,1)S(1)} %copy-done, f32[8]{0:T(128)S(1)} %copy-done.5, f32[128,128]{1,0:T(8,128)S(1)} %bitcast.7, f32[7,128,128]{2,1,0:T(8,128)S(1)} %bitcast.5, f32[7,128,128]{2,1,0:T(8,128)S(1)} %bitcast.6, bf16[6,128,128]{2,1,0:T(8,128)(2,1)S(1)} %copy-done.3), custom_call_target="tpu_custom_call" | custom-call | tf_op jit(solution)/shard_map/pallas_call | solution.py:327
  58.1 0.6 %copy.10 = f32[4,32,128]{2,1,0:T(8,128)} copy(f32[4,32,128]{2,1,0:T(8,128)S(1)} %bitcast.9) | data formatting | bytes 131072
  58.7 0.6 %copy.11 = f32[4,32,128]{2,1,0:T(8,128)} copy(f32[4,32,128]{2,1,0:T(8,128)S(1)} %bitcast.8) | data formatting | bytes 131072
Async XLA Ops:
  0.6 3.4 %copy-start = (bf16[8,128,32,128]{3,2,1,0:T(8,128)(2,1)S(1)}, bf16[8,128,32,128]{3,2,1,0:T(8,128)(2,1)}, u32[]{:S(2)}) copy-start(bf16[8,128,32,128]{3,2,1,0:T(8,128)(2,1)} %orb.1) | copy-start | bytes 25165828
  4.0 1.0 %copy-start.1 = (f32[7,4,32,128]{3,2,1,0:T(8,128)S(1)}, f32[7,4,32,128]{3,2,1,0:T(8,128)}, u32[]{:S(2)}) copy-start(f32[7,4,32,128]{3,2,1,0:T(8,128)} %param.9) | copy-start | bytes 1376260
  5.0 1.0 %copy-start.2 = (f32[7,4,32,128]{3,2,1,0:T(8,128)S(1)}, f32[7,4,32,128]{3,2,1,0:T(8,128)}, u32[]{:S(2)}) copy-start(f32[7,4,32,128]{3,2,1,0:T(8,128)} %param.10) | copy-start | bytes 1376260
  6.1 0.9 %copy-start.3 = (bf16[6,128,128]{2,1,0:T(8,128)(2,1)S(1)}, bf16[6,128,128]{2,1,0:T(8,128)(2,1)}, u32[]{:S(2)}) copy-start(bf16[6,128,128]{2,1,0:T(8,128)(2,1)} %constant.2.clone.tab_h) | copy-start | bytes 589828
  7.0 0.8 %copy-start.4 = (f32[4,32,128]{2,1,0:T(8,128)S(1)}, f32[4,32,128]{2,1,0:T(8,128)}, u32[]{:S(2)}) copy-start(f32[4,32,128]{2,1,0:T(8,128)} %param.8) | copy-start | bytes 196612
  7.8 0.7 %copy-start.5 = (f32[8]{0:T(128)S(1)}, f32[8]{0:T(128)}, u32[]{:S(2)}) copy-start(f32[8]{0:T(128)} %occ.1) | copy-start | bytes 100

commit v2 on v1

v2 whole, which is shorter than its diff:
```python
import functools

import jax
import jax.numpy as jnp
import numpy as np
from jax import lax
from jax.experimental import pallas as pl
from jax.experimental.pallas import tpu as pltpu
from jax.sharding import Mesh
from jax.sharding import PartitionSpec as P

LOGICAL = pl.DeviceIdType.LOGICAL
BAND = ("x", "y", "c")
N = 128
HIST = 7
beta_mix = 0.5
spacing = 0.2
f32 = jnp.float32
bf16 = jnp.bfloat16
STREAMS = (0, 2, 1, 3)
PIECES = [(h, s) for h in range(2) for s in STREAMS]
EARLY = 5
HIST_SENDS = (40, 60)


def tables():
    k = np.arange(N)
    angle = 2.0 * np.pi * ((k[:, None] * k[None, :]) % N) / N
    basis = (np.cos(angle) + np.sin(angle)) / np.sqrt(N)
    order = (4 * np.arange(32)[None, :] + np.arange(4)[:, None]).reshape(-1)
    parts = []
    for table in (basis, basis[:, order], basis[order, :]):
        high = table.astype(jnp.bfloat16)
        low = (table - high.astype(np.float64)).astype(jnp.bfloat16)
        parts += [high, low]
    return jnp.asarray(np.stack(parts))


def halves(value):
    high = value.astype(bf16)
    return high, (value - high.astype(f32)).astype(bf16)


def product(left, right, dims):
    dot = functools.partial(
        lax.dot_general, dimension_numbers=(dims, ((), ())), preferred_element_type=f32
    )
    return dot(left[0], right[0]) + (dot(left[0], right[1]) + dot(left[1], right[0]))


def partner_ids(x, y, c, z):
    plane = {(i, j): ((x + i) % 4) * 32 + ((y + j) % 4) * 8 for i in range(4) for j in range(4)}
    rest = {(i, j): ((c + i) % 2) * 4 + (z + j) % 4 for i in range(2) for j in range(4)}
    slot_plane = {(i, j): ((x + i) % 4) * 8 + ((y + j) % 4) * 2 for i in range(4) for j in range(4)}
    slot_rest = {(i, j): ((c + i) % 2) + ((z + j) % 4) * 32 for i in range(2) for j in range(4)}
    moves = [(a, b, d, e) for a in range(4) for b in range(4) for d in range(2) for e in range(4)][1:]

    def hops(m):
        return sum((0, 1, 2, 1)[m[i]] for i in (0, 1, 3))

    moves.sort(key=lambda m: -hops(m))
    return [
        (plane[m[:2]] + rest[m[2:]], slot_plane[m[:2]] + slot_rest[m[2:]], m) for m in moves
    ]


def regroup(rows):
    block = lax.broadcasted_iota(jnp.int32, (32, N), 1) // 32
    turned = {}
    for i in range(4):
        for j in range(4):
            shift = (i - j) % 4
            if (i, shift) not in turned:
                turned[i, shift] = rows[i] if shift == 0 else pltpu.roll(rows[i], 32 * shift, 1)
    out = []
    for j in range(4):
        value = turned[0, (0 - j) % 4]
        for i in range(1, 4):
            value = jnp.where(block == i, turned[i, (i - j) % 4], value)
        out.append(value)
    return out


def kernel(
    orb, occ, rin_h, hin_h, hres_h, tab_h, rho_h, v_h,
    orb_v, rin, hin, hres, tab, part, crecv, r1, r2, r3,
    hsend, hrecv, xsend, xrecv, vsend, vrecv,
    load_sem, in_sem, c_send, c_recv, rs_send, rs_recv, a_send, a_recv, z_sem,
):
    x, y, c, z = (lax.axis_index(a) for a in ("x", "y", "c", "z"))

    def place(px, py, pc, pz):
        return px * 32 + py * 8 + pc * 4 + pz

    me = place(x, y, c, z)
    my_slot = z * 32 + x * 8 + y * 2 + c
    others = partner_ids(x, y, c, z)

    barrier = pltpu.get_barrier_semaphore()
    near = [t for t, _, m in others if sum(v > 0 for v in m) == 1]
    for t in near:
        pl.semaphore_signal(barrier, inc=1, device_id=t, device_id_type=LOGICAL)

    def load(p):
        h, s = PIECES[p]
        return pltpu.make_async_copy(
            orb.at[:, :, s, pl.ds(h * 16, 16)], orb_v.at[p], load_sem.at[p]
        )

    for p in range(8):
        load(p).start()
    inputs = [(tab_h, tab), (hres_h, hres), (hin_h, hin), (rin_h, rin)]
    for i, (a, b) in enumerate(inputs):
        pltpu.make_async_copy(a, b, in_sem.at[i]).start()

    occupied = [occ[k] for k in range(8)]

    def density(p):
        h, s = PIECES[p]
        load(p).wait()

        @pl.loop(0, 4)
        def _(i):
            for row in range(8):
                total = None
                for k in range(8):
                    value = orb_v[p, k, i * 8 + row].astype(f32)
                    term = occupied[k] * (value * value)
                    total = term if total is None else total + term
                part[h, i, row // 2, row % 2, s] = total

    def c_copy(p):
        h, s = PIECES[p]
        return pltpu.make_async_remote_copy(
            src_ref=part.at[h, :, :, 1 - c, s], dst_ref=crecv.at[h, s],
            send_sem=c_send.at[p], recv_sem=c_recv.at[p],
            device_id=place(x, y, 1 - c, z), device_id_type=LOGICAL,
        )

    with jax.named_scope("density"):
        for p in range(EARLY):
            density(p)
    with jax.named_scope("barrier"):
        pl.semaphore_wait(barrier, len(near))
    with jax.named_scope("density_rest"):
        for p in range(EARLY):
            c_copy(p).start()
        for p in range(EARLY, 8):
            density(p)
            c_copy(p).start()

    flip = {
        "x": {1: x + 1 - 2 * (x % 2), 2: (x + 2) % 4, 3: 3 - x},
        "y": {1: y + 1 - 2 * (y % 2), 2: (y + 2) % 4, 3: 3 - y},
    }
    mine = {"x": x, "y": y}
    orders = {0: ("x", "y", 1), 1: ("x", "y", 3), 2: ("y", "x", 1), 3: ("y", "x", 3)}

    def dev(axis, e):
        if axis == "x":
            return place(flip["x"][e], y, c, z)
        return place(x, flip["y"][e], c, z)

    def steps(p):
        h, s = PIECES[p]
        first, second, e1 = orders[s]
        e2 = 4 - e1

        def remote(src, dst, sem, to):
            return pltpu.make_async_remote_copy(
                src_ref=src, dst_ref=dst, send_sem=rs_send.at[p * 6 + sem],
                recv_sem=rs_recv.at[p * 6 + sem], device_id=to, device_id_type=LOGICAL,
            )

        def rows_of(index):
            if first == "x":
                return part.at[h, index, :, c, s]
            return part.at[h, :, index, c, s]

        def block_of(index):
            if second == "x":
                return part.at[h, index, y, c, s]
            return part.at[h, x, index, c, s]

        one = [
            (remote(rows_of(flip[first][e1]), r1.at[h, s, 0], 0, dev(first, e1)),
             rows_of(mine[first]), r1.at[h, s, 0]),
            (remote(rows_of(flip[first][2]), r1.at[h, s, 1], 1, dev(first, e1)),
             rows_of(flip[first][e2]), r1.at[h, s, 1]),
        ]
        two = [
            (remote(rows_of(flip[first][e2]), r2.at[h, s], 2, dev(first, e2)),
             rows_of(mine[first]), r2.at[h, s]),
        ]
        three = [
            (remote(block_of(flip[second][e]), r3.at[h, s, e - 1], 2 + e, dev(second, e)),
             block_of(mine[second]), r3.at[h, s, e - 1])
            for e in (2, 1, 3)
        ]
        return [one, two, three]

    plan = [steps(p) for p in range(8)]

    def begin(p, step):
        for copy, _, _ in plan[p][step]:
            copy.start()

    def take(p, step):
        for copy, into, came in plan[p][step]:
            copy.wait_recv()
            into[...] = into[...] + came[...]

    with jax.named_scope("core_sum"):
        for p in range(8):
            h, s = PIECES[p]
            c_copy(p).wait_recv()
            own = part.at[h, :, :, c, s]
            own[...] = own[...] + crecv[h, s]
            begin(p, 0)
        for e in (1, 2, 3):
            pl.semaphore_signal(
                z_sem, inc=1, device_id=place(x, y, c, (z + e) % 4), device_id_type=LOGICAL
            )

    lane = lax.broadcasted_iota(jnp.int32, (8, N), 1)
    sub = lax.broadcasted_iota(jnp.int32, (8, N), 0)

    def fold(value):
        return jnp.sum(value.reshape(16, 8, N), axis=0)

    def products(field, amount):
        rows = jnp.zeros((8, N), f32)
        for j in range(amount):
            line = jnp.sum(fold(field * hres[j]), axis=0, keepdims=True)
            rows = jnp.where(sub == j, line, rows)
        return rows

    def placed(i, rows):
        total = jnp.sum(rows, axis=1, keepdims=True)
        spots = (lane == 8 * i + sub) | (lane == 8 * sub + i)
        return jnp.sum(jnp.where(spots & (sub <= i), total, 0.0), axis=0, keepdims=True)

    def every(start, count=N):
        return pl.ds(start, count, stride=8)

    with jax.named_scope("hist"):
        for i, (a, b) in enumerate(inputs):
            pltpu.make_async_copy(a, b, in_sem.at[i]).wait()
        basis = (tab[0], tab[1])
        for m in range(HIST):
            trial = hin[m] + beta_mix * hres[m]
            hsend[every(m), :] = product(basis, halves(trial), ((1,), (1,)))
        row = jnp.zeros((1, N), f32)
        for i in range(HIST):
            row = row + placed(i, products(hres[i], i + 1))
        hsend[every(7), :] = jnp.broadcast_to(row, (N, N))

    with jax.named_scope("step1"):
        for p in range(8):
            take(p, 0)
            if p == 0:
                pl.semaphore_wait(z_sem, 3)
            begin(p, 1)

    def exchange(pairs, source, target, sem):
        for t, slot, _ in pairs:
            pltpu.make_async_remote_copy(
                src_ref=source(t, slot), dst_ref=target,
                send_sem=a_send.at[sem], recv_sem=a_recv.at[sem],
                device_id=t, device_id_type=LOGICAL,
            ).start()

    def arrived(buffer, rows, sem):
        whole = buffer.at[pl.ds(0, 127 * rows)]
        pltpu.make_async_copy(whole, whole, a_recv.at[sem]).wait()

    def sent(buffer, rows, sem):
        whole = buffer.at[pl.ds(0, 127 * rows)]
        pltpu.make_async_copy(whole, whole, a_send.at[sem]).wait()

    def tile(index, rows):
        return pl.ds(pl.multiple_of(index * 8, 8), rows)

    def hist_exchange(pairs):
        exchange(pairs, lambda t, slot: hsend.at[tile(t, 8)], hrecv.at[tile(my_slot, 8)], 0)

    def unheard(o):
        return o[2][0] == 2 and o[2][1] == 2 and o[2][3] > 0

    hist_order = [o for o in others if not unheard(o)] + [o for o in others if unheard(o)]
    first, second = HIST_SENDS
    with jax.named_scope("step2a"):
        for p in range(4):
            take(p, 1)
            begin(p, 2)
    with jax.named_scope("hist_send1"):
        hist_exchange(hist_order[:first])
        hrecv[tile(my_slot, 8), :] = hsend[tile(me, 8), :]
    with jax.named_scope("step2b"):
        for p in range(4, 8):
            take(p, 1)
            begin(p, 2)
    with jax.named_scope("hist_send2"):
        hist_exchange(hist_order[first : first + second])
    with jax.named_scope("step3"):
        for p in range(8):
            take(p, 2)

    with jax.named_scope("new"):
        blocks = [part[h, x, y, c, s] for s in range(4) for h in range(2)]
        new = jnp.concatenate(blocks, axis=0) - rin[...]
        xsend[every(0), :] = product(basis, halves(rin[...] + beta_mix * new), ((1,), (1,)))
        rows = products(new, HIST)
        rows = jnp.where(sub == 7, jnp.sum(fold(new * new), axis=0, keepdims=True), rows)
        row = placed(7, rows)
        xsend[every(1), :] = jnp.broadcast_to(row, (N, N))
    with jax.named_scope("x_send"):
        exchange(others, lambda t, slot: xsend.at[tile(t, 2)], xrecv.at[tile(my_slot, 2)], 1)
        xrecv[tile(my_slot, 2), :] = xsend[tile(me, 2), :]
    with jax.named_scope("hist_send3"):
        hist_exchange(hist_order[first + second :])

    with jax.named_scope("coulomb"):
        p_index = lax.broadcasted_iota(jnp.int32, (N, N), 0)
        q_index = lax.broadcasted_iota(jnp.int32, (N, N), 1)
        freq_p = jnp.minimum(p_index, N - p_index)
        freq_q = jnp.minimum(q_index, N - q_index)
        freq_r = jnp.minimum(me, N - me)
        squared = freq_p * freq_p + freq_q * freq_q + freq_r * freq_r
        cell = N * spacing
        floored = jnp.maximum(squared, 1).astype(f32)
        coulomb = jnp.where(squared > 0, cell * cell / np.pi / floored, 0.0)

    with jax.named_scope("hist_wait"):
        arrived(hrecv, 8, 0)
    with jax.named_scope("x_wait"):
        arrived(xrecv, 2, 1)

    with jax.named_scope("solve"):
        flat = jnp.sum(xrecv[every(1), :], axis=0, keepdims=True)
        flat = (flat + jnp.sum(hrecv[every(7), :], axis=0, keepdims=True)) * (1.0 / (N * N * N))
        matrix = jnp.zeros((8, N), f32)
        for i in range(8):
            shifted = flat if i == 0 else pltpu.roll(flat, N - 8 * i, 1)
            matrix = jnp.where(sub == i, shifted, matrix)
        matrix = jnp.where(lane < 8, matrix, jnp.where(lane == 8, 1.0, 0.0))
        for k in range(8):
            pivot_row = matrix[k : k + 1, :]
            column = jnp.sum(jnp.where(lane == k, matrix, 0.0), axis=1, keepdims=True)
            pivot = column[k : k + 1, :]
            matrix = jnp.where(sub == k, matrix, matrix - (column / pivot) * pivot_row)
        diagonal = jnp.sum(jnp.where(lane == sub, matrix, 0.0), axis=1, keepdims=True)
        right = jnp.sum(jnp.where(lane == 8, matrix, 0.0), axis=1, keepdims=True)
        solved = right / diagonal
        weights = solved / jnp.sum(solved, axis=0, keepdims=True)

    with jax.named_scope("planes"):
        plane = weights[7:8, :] * xrecv[every(0), :]
        for m in range(HIST):
            plane = plane + weights[m : m + 1, :] * hrecv[every(m), :]
        grouped = jnp.concatenate(regroup([plane[g * 32 : (g + 1) * 32] for g in range(4)]), axis=0)
        second = product(halves(grouped), basis, ((1,), (0,)))
        spectrum = product((tab[2], tab[3]), halves(second), ((1,), (0,))) * coulomb
        back = product((tab[4], tab[5]), halves(spectrum), ((1,), (0,)))
        back = product(halves(back), basis, ((1,), (0,)))
        back = regroup([back[a * 32 : (a + 1) * 32] for a in range(4)])
        vsend[...] = jnp.concatenate(back, axis=0)
    with jax.named_scope("v_send"):
        exchange(others, lambda t, slot: vsend.at[pl.ds(slot, 1)], vrecv.at[pl.ds(me, 1)], 2)
        vrecv[pl.ds(me, 1)] = vsend[pl.ds(my_slot, 1)]

    with jax.named_scope("mix"):
        rho = weights[7:8, :] * (rin[...] + beta_mix * new)
        for m in range(HIST):
            rho = rho + weights[m : m + 1, :] * (hin[m] + beta_mix * hres[m])
        rho_h[...] = rho
        for p in range(8):
            c_copy(p).wait_send()
            for step in plan[p]:
                for copy, _, _ in step:
                    copy.wait_send()
        sent(hsend, 8, 0)
        sent(xsend, 2, 1)

    with jax.named_scope("v_wait"):
        arrived(vrecv, 1, 2)
    with jax.named_scope("last"):
        v_h[...] = product(halves(vrecv[...].T), basis, ((1,), (0,)))
    sent(vsend, 1, 2)


def local(orbitals, occupations, rho_in, hist_in, hist_res):
    anywhere = pl.BlockSpec(memory_space=pl.ANY)
    vmem, dma = pltpu.VMEM, pltpu.SemaphoreType.DMA
    square = (N, N)
    rho, v = pl.pallas_call(
        kernel,
        out_shape=[jax.ShapeDtypeStruct(square, f32)] * 2,
        in_specs=[anywhere, pl.BlockSpec(memory_space=pltpu.SMEM)] + [anywhere] * 4,
        out_specs=[pl.BlockSpec(memory_space=pltpu.VMEM)] * 2,
        scratch_shapes=[
            vmem((8, 8, 32, 16, N), bf16), vmem(square, f32), vmem((HIST, N, N), f32),
            vmem((HIST, N, N), f32), vmem((6, N, N), bf16),
            vmem((2, 4, 4, 2, 4, 16, N), f32), vmem((2, 4, 4, 4, 16, N), f32),
            vmem((2, 4, 2, 4, 16, N), f32), vmem((2, 4, 4, 16, N), f32),
            vmem((2, 4, 3, 16, N), f32),
            vmem((8 * N, N), f32), vmem((8 * N, N), f32), vmem((8 * N, N), f32),
            vmem((8 * N, N), f32), vmem(square, f32), vmem(square, f32),
            dma((8,)), dma((4,)), dma((8,)), dma((8,)),
            dma((48,)), dma((48,)), dma((3,)), dma((3,)), pltpu.SemaphoreType.REGULAR,
        ],
        compiler_params=pltpu.CompilerParams(
            collective_id=0, has_side_effects=True, vmem_limit_bytes=67043328
        ),
    )(
        orbitals.reshape(8, 32, 4, 32, N), occupations, rho_in.reshape(square),
        hist_in.reshape(HIST, N, N), hist_res.reshape(HIST, N, N), tables(),
    )
    return rho.reshape(rho_in.shape), v.reshape(rho_in.shape)


def solution(mesh):
    finer = Mesh(mesh.devices.reshape(4, 4, 2, 4), ("x", "y", "c", "z"))
    in_specs = (
        P(BAND, None, "z", None), P(BAND), P(BAND, "z", None),
        P(None, BAND, "z", None), P(None, BAND, "z", None),
    )
    out_specs = (P(BAND, "z", None), P(BAND, "z", None))
    return jax.shard_map(local, mesh=finer, in_specs=in_specs, out_specs=out_specs, check_vma=False)
```

time: 59.7 us -> 45.9 us (0.77)
  Pallas kernels: 49.6 us -> 42.1 us
  local copies, waits for them, and re-layouts: 9.09 us -> 2.95 us
    pallas_call x1, Pallas kernels: 49.6 us -> 42.1 us  [local(): pl.pallas_call(kernel, out_shape=[jax.ShapeDtypeStruct(square, f32)] * 2,...]
    unnamed x14 -> x2, local copies, waits for them, and re-layouts: 9.09 us -> 2.95 us
where the time goes in v2:
time: 45.9 us; the launch traced here: 45.7 us
  Pallas kernels  42.1 us (92%)
  local copies, waits for them, and re-layouts  2.95 us (6%)
  between operations  0.64 us (1%)
    pallas_call x1, Pallas kernels, local(): pl.pallas_call(kernel, out_shape=[jax.ShapeDtypeStruct(square, f32)] * 2,...  42.1 us
    unnamed x2, local copies, waits for them, and re-layouts  2.95 us

profile of v2, /device:TPU:1, one launch (start us, length us, event | category | flops | bytes accessed | tf_op | source)
XLA Modules:
  0.0 45.7 jit_solution(1781747005929545482)
XLA Ops:
  0.6 42.1 %shard_map.77 = (f32[128,128]{1,0:T(8,128)}, f32[128,128]{1,0:T(8,128)}) custom-call(bf16[8,32,4,32,128]{4,3,2,1,0:T(8,128)(2,1)} %bitcast.6, f32[8]{0:T(128)} %occ.1, f32[128,128]{1,0:T(8,128)} %bitcast.9, f32[7,128,128]{2,1,0:T(8,128)} %bitcast.7, f32[7,128,128]{2,1,0:T(8,128)} %bitcast.8, bf16[6,128,128]{2,1,0:T(8,128)(2,1)} %constant.2.clone.tab_h), custom_call_target="tpu_custom_call" | custom-call | tf_op jit(solution)/shard_map/pallas_call | solution.py:396
  42.7 1.5 %copy.10 = f32[4,32,128]{2,1,0:T(8,128)} copy(f32[4,32,128]{2,1,0:T(8,128)} %bitcast.11) | data formatting | bytes 131072
  44.2 1.5 %copy.11 = f32[4,32,128]{2,1,0:T(8,128)} copy(f32[4,32,128]{2,1,0:T(8,128)} %bitcast.10) | data formatting | bytes 131072

commit v3 on v2

v3 whole, which is shorter than its diff:
```python
import functools

import jax
import jax.numpy as jnp
import numpy as np
from jax import lax
from jax.experimental import pallas as pl
from jax.experimental.pallas import tpu as pltpu
from jax.sharding import Mesh
from jax.sharding import PartitionSpec as P

LOGICAL = pl.DeviceIdType.LOGICAL
BAND = ("x", "y", "c")
N = 128
HIST = 7
beta_mix = 0.5
spacing = 0.2
f32 = jnp.float32
bf16 = jnp.bfloat16
STREAMS = (0, 2, 1, 3)
PARTS = 4
ROWS = 32 // PARTS
PIECES = [(h, s) for h in range(2) for s in STREAMS]
SENDS = [(h, s) for h in range(PARTS) for s in STREAMS]
EARLY = 1
LAG = 4
STAGES = (0, 0, 0, 119)
REST_AT = 2


def tables():
    k = np.arange(N)
    angle = 2.0 * np.pi * ((k[:, None] * k[None, :]) % N) / N
    basis = (np.cos(angle) + np.sin(angle)) / np.sqrt(N)
    order = (4 * np.arange(32)[None, :] + np.arange(4)[:, None]).reshape(-1)
    parts = []
    for table in (basis, basis[:, order], basis[order, :]):
        high = table.astype(jnp.bfloat16)
        low = (table - high.astype(np.float64)).astype(jnp.bfloat16)
        parts += [high, low]
    return jnp.asarray(np.stack(parts))


def halves(value):
    high = value.astype(bf16)
    return high, (value - high.astype(f32)).astype(bf16)


def product(left, right, dims):
    dot = functools.partial(
        lax.dot_general, dimension_numbers=(dims, ((), ())), preferred_element_type=f32
    )
    return dot(left[0], right[0]) + (dot(left[0], right[1]) + dot(left[1], right[0]))


def partner_ids(x, y, c, z):
    plane = {(i, j): ((x + i) % 4) * 32 + ((y + j) % 4) * 8 for i in range(4) for j in range(4)}
    rest = {(i, j): ((c + i) % 2) * 4 + (z + j) % 4 for i in range(2) for j in range(4)}
    slot_plane = {(i, j): ((x + i) % 4) * 8 + ((y + j) % 4) * 2 for i in range(4) for j in range(4)}
    slot_rest = {(i, j): ((c + i) % 2) + ((z + j) % 4) * 32 for i in range(2) for j in range(4)}
    moves = [(a, b, d, e) for a in range(4) for b in range(4) for d in range(2) for e in range(4)][1:]

    def hops(m):
        return sum((0, 1, 2, 1)[m[i]] for i in (0, 1, 3))

    moves.sort(key=lambda m: -hops(m))
    return [
        (plane[m[:2]] + rest[m[2:]], slot_plane[m[:2]] + slot_rest[m[2:]], m) for m in moves
    ]


def regroup(rows):
    block = lax.broadcasted_iota(jnp.int32, (32, N), 1) // 32
    turned = {}
    for i in range(4):
        for j in range(4):
            shift = (i - j) % 4
            if (i, shift) not in turned:
                turned[i, shift] = rows[i] if shift == 0 else pltpu.roll(rows[i], 32 * shift, 1)
    out = []
    for j in range(4):
        value = turned[0, (0 - j) % 4]
        for i in range(1, 4):
            value = jnp.where(block == i, turned[i, (i - j) % 4], value)
        out.append(value)
    return out


def kernel(
    orb, occ_h, rin_h, hin_h, hres_h, tab_h, rho_h, v_h,
    orb_v, occ, rin, hin, hres, tab, part, crecv, r1, r2,
    hsend, hrecv, xsend, xrecv, vsend, vrecv,
    load_sem, in_sem, c_recv, r_send, rs_recv, a_send, a_recv, z_sem,
):
    x, y, c, z = (lax.axis_index(a) for a in ("x", "y", "c", "z"))

    def place(px, py, pc, pz):
        return px * 32 + py * 8 + pc * 4 + pz

    me = place(x, y, c, z)
    my_slot = z * 32 + x * 8 + y * 2 + c
    def load(p):
        h, s = PIECES[p]
        return pltpu.make_async_copy(
            orb.at[:, :, s, pl.ds(h * 16, 16)], orb_v.at[p], load_sem.at[p]
        )

    occ_copy = pltpu.make_async_copy(occ_h, occ, in_sem.at[4])
    occ_copy.start()
    load(0).start()
    barrier = pltpu.get_barrier_semaphore()
    near = [place(x, y, 1 - c, z)]
    for e in (2, 1, 3):
        near += [
            place((x + e) % 4, y, c, z), place(x, (y + e) % 4, c, z), place(x, y, c, (z + e) % 4)
        ]
    for t in near:
        pl.semaphore_signal(barrier, inc=1, device_id=t, device_id_type=LOGICAL)
    for p in range(1, 8):
        load(p).start()
    inputs = [(tab_h, tab), (hres_h, hres), (hin_h, hin), (rin_h, rin)]
    for i, (a, b) in enumerate(inputs):
        pltpu.make_async_copy(a, b, in_sem.at[i]).start()

    occ_copy.wait()
    occupied = [occ[k] for k in range(8)]

    def density(p):
        h, s = PIECES[p]
        load(p).wait()

        @pl.loop(0, 4)
        def _(i):
            for row in range(8):
                total = None
                for k in range(8):
                    value = orb_v[p, k, i * 8 + row].astype(f32)
                    term = occupied[k] * (value * value)
                    total = term if total is None else total + term
                for k in range(PARTS // 2):
                    part[h * (PARTS // 2) + k, i, row // 2, row % 2, s] = total[
                        k * ROWS : (k + 1) * ROWS
                    ]

    def c_copy(p):
        h, s = SENDS[p]
        return pltpu.make_async_remote_copy(
            src_ref=part.at[h, :, :, 1 - c, s], dst_ref=crecv.at[h, s],
            send_sem=r_send.at[0], recv_sem=c_recv.at[PIECES.index((h // (PARTS // 2), s))],
            device_id=place(x, y, 1 - c, z), device_id_type=LOGICAL,
        )

    def c_begin(p):
        h, s = PIECES[p]
        for k in range(PARTS // 2):
            c_copy(SENDS.index((h * (PARTS // 2) + k, s))).start()

    flip = {
        "x": {1: x + 1 - 2 * (x % 2), 2: (x + 2) % 4, 3: 3 - x},
        "y": {1: y + 1 - 2 * (y % 2), 2: (y + 2) % 4, 3: 3 - y},
    }
    mine = {"x": x, "y": y}
    orders = {0: ("x", "y", 1), 1: ("x", "y", 3), 2: ("y", "x", 1), 3: ("y", "x", 3)}

    def dev(axis, e):
        if axis == "x":
            return place(flip["x"][e], y, c, z)
        return place(x, flip["y"][e], c, z)

    def steps(p):
        h, s = SENDS[p]
        first, second, e1 = orders[s]
        e2 = 4 - e1

        def remote(src, dst, sem, to):
            return pltpu.make_async_remote_copy(
                src_ref=src, dst_ref=dst, send_sem=r_send.at[1 + sem],
                recv_sem=rs_recv.at[PARTS * sem + h], device_id=to, device_id_type=LOGICAL,
            )

        def rows_of(index):
            if first == "x":
                return part.at[h, index, :, c, s]
            return part.at[h, :, index, c, s]

        def spot(i, j):
            return (i, j) if first == "x" else (j, i)

        one = [
            (remote(rows_of(flip[first][e1]), r1.at[h, s, 0], 0, dev(first, e1)),
             rows_of(mine[first]), r1.at[h, s, 0]),
            (remote(rows_of(flip[first][2]), r1.at[h, s, 1], 0, dev(first, e1)),
             rows_of(flip[first][e2]), r1.at[h, s, 1]),
        ]
        two = []
        moves = [(e2, 2), (e2, 1), (e2, 3), (0, 2), (e2, 0), (0, 1), (0, 3)]
        for n, (i, j) in enumerate(moves):
            to_x, to_y = spot(
                flip[first][i] if i else mine[first], flip[second][j] if j else mine[second]
            )
            two.append(remote(
                part.at[h, to_x, to_y, c, s], r2.at[h, s, n], 1, place(to_x, to_y, c, z)
            ))
        return one, two

    plan = [steps(p) for p in range(4 * PARTS)]

    def bytes_of(ref, sem):
        pltpu.make_async_copy(ref, ref, sem).wait()

    def core_sum(p):
        half, s = PIECES[p]
        inner = PARTS // 2
        bytes_of(crecv.at[pl.ds(half * inner, inner), s], c_recv.at[p])
        for h in range(half * inner, (half + 1) * inner):
            own = part.at[h, :, :, c, s]
            own[...] = own[...] + crecv[h, s]
            for copy, _, _ in plan[SENDS.index((h, s))][0]:
                copy.start()

    others = partner_ids(x, y, c, z)

    for p in range(8):
        with jax.named_scope(f"density_{p}"):
            density(p)
        if p == EARLY - 1:
            with jax.named_scope("barrier"):
                pl.semaphore_wait(barrier, len(near))
            for q in range(EARLY):
                c_begin(q)
        elif p >= EARLY:
            c_begin(p)
        if p - LAG >= 0 and p >= EARLY:
            with jax.named_scope(f"core_{p}"):
                core_sum(p - LAG)
    with jax.named_scope("core_rest"):
        for p in range(8 - LAG, 8):
            core_sum(p)

    lane = lax.broadcasted_iota(jnp.int32, (8, N), 1)
    sub = lax.broadcasted_iota(jnp.int32, (8, N), 0)

    def fold(value):
        return jnp.sum(value.reshape(16, 8, N), axis=0)

    def products(field, amount):
        rows = jnp.zeros((8, N), f32)
        for j in range(amount):
            line = jnp.sum(fold(field * hres[j]), axis=0, keepdims=True)
            rows = jnp.where(sub == j, line, rows)
        return rows

    def placed(i, rows):
        total = jnp.sum(rows, axis=1, keepdims=True)
        spots = (lane == 8 * i + sub) | (lane == 8 * sub + i)
        return jnp.sum(jnp.where(spots & (sub <= i), total, 0.0), axis=0, keepdims=True)

    def every(start, count=N):
        return pl.ds(start, count, stride=8)

    with jax.named_scope("hist"):
        for i, (a, b) in enumerate(inputs):
            pltpu.make_async_copy(a, b, in_sem.at[i]).wait()
        basis = (tab[0], tab[1])
        for m in range(HIST):
            trial = hin[m] + beta_mix * hres[m]
            hsend[every(m), :] = product(basis, halves(trial - 1.0), ((1,), (1,)))
        row = jnp.zeros((1, N), f32)
        for i in range(HIST):
            row = row + placed(i, products(hres[i], i + 1))
        early_row = row

    def exchange(pairs, source, target, sem):
        for t, slot, _ in pairs:
            pltpu.make_async_remote_copy(
                src_ref=source(t, slot), dst_ref=target,
                send_sem=a_send.at[sem], recv_sem=a_recv.at[sem],
                device_id=t, device_id_type=LOGICAL,
            ).start()

    def arrived(buffer, rows, sem):
        whole = buffer.at[pl.ds(0, 127 * rows)]
        pltpu.make_async_copy(whole, whole, a_recv.at[sem]).wait()

    def sent(buffer, rows, sem):
        whole = buffer.at[pl.ds(0, 127 * rows)]
        pltpu.make_async_copy(whole, whole, a_send.at[sem]).wait()

    def tile(index, rows):
        return pl.ds(pl.multiple_of(index * 8, 8), rows)

    def hist_exchange(pairs):
        exchange(pairs, lambda t, slot: hsend.at[tile(t, 7)], hrecv.at[tile(my_slot, 7)], 0)

    def unheard(o):
        return o[2][0] == 2 and o[2][1] == 2

    hist_order = sorted(others, key=lambda o: (unheard(o), o[2][3] > 0))
    ends = np.cumsum((0,) + STAGES)
    def hist_stage(h):
        if h == 0:
            hrecv[tile(my_slot, 7), :] = hsend[tile(me, 7), :]
        with jax.named_scope(f"hist_send{h}"):
            if ends[h] <= 29 < ends[h + 1]:
                pl.semaphore_wait(z_sem, 3)
            hist_exchange(hist_order[ends[h] : ends[h + 1]])

    for h in range(PARTS):
        with jax.named_scope(f"step1_{h}"):
            bytes_of(r1.at[h], rs_recv.at[h])
            for p in range(4 * h, 4 * h + 4):
                for _, into, came in plan[p][0]:
                    into[...] = into[...] + came[...]
            if h == 0:
                for e in (1, 2, 3):
                    pl.semaphore_signal(
                        z_sem, inc=1, device_id=place(x, y, c, (z + e) % 4), device_id_type=LOGICAL
                    )
            for p in range(4 * h, 4 * h + 4):
                for copy in plan[p][1]:
                    copy.start()
        hist_stage(h)

    for h in range(PARTS):
        with jax.named_scope(f"step2_{h}"):
            bytes_of(r2.at[h], rs_recv.at[PARTS + h])
            if h == REST_AT:
                hist_exchange(hist_order[ends[-1] :])

    with jax.named_scope("new"):
        blocks = []
        for s in range(4):
            for h in range(PARTS):
                total = part[h, x, y, c, s]
                for n in range(7):
                    total = total + r2[h, s, n]
                blocks.append(total)
        new = jnp.concatenate(blocks, axis=0) - rin[...]
        xsend[every(0), :] = product(basis, halves((rin[...] - 1.0) + beta_mix * new), ((1,), (1,)))
        rows = products(new, HIST)
        rows = jnp.where(sub == 7, jnp.sum(fold(new * new), axis=0, keepdims=True), rows)
        row = early_row + placed(7, rows)
        xsend[every(1), :] = jnp.broadcast_to(row, (N, N))
    with jax.named_scope("x_send"):
        exchange(others, lambda t, slot: xsend.at[tile(t, 2)], xrecv.at[tile(my_slot, 2)], 1)
        xrecv[tile(my_slot, 2), :] = xsend[tile(me, 2), :]
    with jax.named_scope("coulomb"):
        p_index = lax.broadcasted_iota(jnp.int32, (N, N), 0)
        q_index = lax.broadcasted_iota(jnp.int32, (N, N), 1)
        freq_p = jnp.minimum(p_index, N - p_index)
        freq_q = jnp.minimum(q_index, N - q_index)
        freq_r = jnp.minimum(me, N - me)
        squared = freq_p * freq_p + freq_q * freq_q + freq_r * freq_r
        cell = N * spacing
        floored = jnp.maximum(squared, 1).astype(f32)
        coulomb = jnp.where(squared > 0, cell * cell / np.pi / floored, 0.0)

    with jax.named_scope("x_wait"):
        arrived(xrecv, 2, 1)
    with jax.named_scope("hist_wait"):
        arrived(hrecv, 7, 0)

    with jax.named_scope("solve"):
        flat = jnp.sum(xrecv[every(1), :], axis=0, keepdims=True)
        flat = flat * (1.0 / (N * N * N))
        entry = {
            (i, j): jnp.broadcast_to(flat[:, 8 * i + j : 8 * i + j + 1], (8, N))
            for i in range(8) for j in range(i + 1)
        }
        right = [jnp.ones((8, N), f32) for _ in range(8)]
        inverse = []
        for k in range(8):
            inverse.append(1.0 / entry[k, k])
            ratio = {i: entry[i, k] * inverse[k] for i in range(k + 1, 8)}
            for i in range(k + 1, 8):
                right[i] = right[i] - ratio[i] * right[k]
                for j in range(k + 1, i + 1):
                    entry[i, j] = entry[i, j] - ratio[i] * entry[j, k]
            for i in range(k + 1, 8):
                entry[i, k] = ratio[i]
        solved = [right[k] * inverse[k] for k in range(8)]
        for k in range(7, -1, -1):
            for i in range(k):
                solved[i] = solved[i] - entry[k, i] * solved[k]
        total = functools.reduce(lambda a, b: a + b, solved)
        weights = [(value / total)[:1] for value in solved]

    with jax.named_scope("planes"):
        plane = weights[7] * xrecv[every(0), :]
        for m in range(HIST):
            plane = plane + weights[m] * hrecv[every(m), :]
        grouped = jnp.concatenate(regroup([plane[g * 32 : (g + 1) * 32] for g in range(4)]), axis=0)
        second = product(halves(grouped), basis, ((1,), (0,)))
        spectrum = product((tab[2], tab[3]), halves(second), ((1,), (0,))) * coulomb
        back = product((tab[4], tab[5]), halves(spectrum), ((1,), (0,)))
        back = product(halves(back), basis, ((1,), (0,)))
        back = regroup([back[a * 32 : (a + 1) * 32] for a in range(4)])
        vsend[...] = jnp.concatenate(back, axis=0)
    with jax.named_scope("v_send"):
        exchange(others, lambda t, slot: vsend.at[pl.ds(slot, 1)], vrecv.at[pl.ds(me, 1)], 2)
        vrecv[pl.ds(me, 1)] = vsend[pl.ds(my_slot, 1)]

    with jax.named_scope("mix"):
        rho = weights[7] * (rin[...] + beta_mix * new)
        for m in range(HIST):
            rho = rho + weights[m] * (hin[m] + beta_mix * hres[m])
        rho_h[...] = rho
    with jax.named_scope("drain"):
        bytes_of(crecv, r_send.at[0])
        bytes_of(r1, r_send.at[1])
        bytes_of(r2, r_send.at[2])
        sent(hsend, 7, 0)
        sent(xsend, 2, 1)

    with jax.named_scope("v_wait"):
        arrived(vrecv, 1, 2)
    with jax.named_scope("last"):
        v_h[...] = product(halves(vrecv[...].T), basis, ((1,), (0,)))
    sent(vsend, 1, 2)


def local(orbitals, occupations, rho_in, hist_in, hist_res):
    anywhere = pl.BlockSpec(memory_space=pl.ANY)
    vmem, dma = pltpu.VMEM, pltpu.SemaphoreType.DMA
    square = (N, N)
    rho, v = pl.pallas_call(
        kernel,
        out_shape=[pltpu.VMEM(square, f32)] * 2,
        in_specs=[anywhere] * 6,
        out_specs=[pl.BlockSpec(memory_space=pltpu.VMEM)] * 2,
        scratch_shapes=[
            vmem((8, 8, 32, 16, N), bf16), pltpu.SMEM((8,), f32), vmem(square, f32), vmem((HIST, N, N), f32),
            vmem((HIST, N, N), f32), vmem((6, N, N), bf16),
            vmem((PARTS, 4, 4, 2, 4, ROWS, N), f32), vmem((PARTS, 4, 4, 4, ROWS, N), f32),
            vmem((PARTS, 4, 2, 4, ROWS, N), f32), vmem((PARTS, 4, 7, ROWS, N), f32),
            vmem((8 * N, N), f32), vmem((8 * N, N), f32), vmem((8 * N, N), f32),
            vmem((8 * N, N), f32), vmem(square, f32), vmem(square, f32),
            dma((8,)), dma((5,)), dma((8,)), dma((3,)), dma((2 * PARTS,)), dma((3,)), dma((3,)), pltpu.SemaphoreType.REGULAR,
        ],
        compiler_params=pltpu.CompilerParams(
            collective_id=0, has_side_effects=True, vmem_limit_bytes=67043328 - 163840
        ),
    )(
        orbitals.reshape(8, 32, 4, 32, N), occupations, rho_in.reshape(square),
        hist_in.reshape(HIST, N, N), hist_res.reshape(HIST, N, N), tables(),
    )
    return rho.reshape(rho_in.shape), v.reshape(rho_in.shape)


def solution(mesh):
    finer = Mesh(mesh.devices.reshape(4, 4, 2, 4), ("x", "y", "c", "z"))
    in_specs = (
        P(BAND, None, "z", None), P(BAND), P(BAND, "z", None),
        P(None, BAND, "z", None), P(None, BAND, "z", None),
    )
    out_specs = (P(BAND, "z", None), P(BAND, "z", None))
    return jax.shard_map(local, mesh=finer, in_specs=in_specs, out_specs=out_specs, check_vma=False)
```

time: 45.9 us -> 38 us (0.83)
  Pallas kernels: 42.1 us -> 36 us
  local copies, waits for them, and re-layouts: 2.95 us -> 1.26 us
    pallas_call x1, Pallas kernels: 42.1 us -> 36 us  [local(): pl.pallas_call(kernel, out_shape=[pltpu.VMEM(square, f32)] * 2, in_specs=...]
    unnamed x2, local copies, waits for them, and re-layouts: 2.95 us -> 1.26 us
where the time goes in v3:
time: 38 us; the launch traced here: 37.9 us
  Pallas kernels  36 us (95%)
  local copies, waits for them, and re-layouts  1.26 us (3%)
  between operations  0.64 us (2%)
    pallas_call x1, Pallas kernels, local(): pl.pallas_call(kernel, out_shape=[pltpu.VMEM(square, f32)] * 2, in_specs=...  36 us
    unnamed x2, local copies, waits for them, and re-layouts  1.26 us

profile of v3, /device:TPU:1, one launch (start us, length us, event | category | flops | bytes accessed | tf_op | source)
XLA Modules:
  0.0 37.9 jit_solution(6362099912970101061)
XLA Ops:
  0.6 36.0 %shard_map.77 = (f32[128,128]{1,0:T(8,128)S(1)}, f32[128,128]{1,0:T(8,128)S(1)}) custom-call(bf16[8,32,4,32,128]{4,3,2,1,0:T(8,128)(2,1)} %bitcast.8, f32[8]{0:T(128)} %occ_h.1, f32[128,128]{1,0:T(8,128)} %bitcast.11, f32[7,128,128]{2,1,0:T(8,128)} %bitcast.9, f32[7,128,128]{2,1,0:T(8,128)} %bitcast.10, bf16[6,128,128]{2,1,0:T(8,128)(2,1)} %constant.2.clone.tab_h), custom_call_target="tpu_custom_call" | custom-call | tf_op jit(solution)/shard_map/pallas_call | solution.py:426
  36.6 0.6 %copy.10 = f32[4,32,128]{2,1,0:T(8,128)} copy(f32[4,32,128]{2,1,0:T(8,128)S(1)} %bitcast.7) | data formatting | bytes 131072
  37.3 0.6 %copy.11 = f32[4,32,128]{2,1,0:T(8,128)} copy(f32[4,32,128]{2,1,0:T(8,128)S(1)} %bitcast.6) | data formatting | bytes 131072

commit v4 on v3

--- a/solution.py
+++ b/solution.py
@@ -23,7 +23,7 @@
 PIECES = [(h, s) for h in range(2) for s in STREAMS]
 SENDS = [(h, s) for h in range(PARTS) for s in STREAMS]
 EARLY = 1
-LAG = 4
+LAG = 5
 STAGES = (0, 0, 0, 119)
 REST_AT = 2
 
@@ -32,12 +32,16 @@
     k = np.arange(N)
     angle = 2.0 * np.pi * ((k[:, None] * k[None, :]) % N) / N
     basis = (np.cos(angle) + np.sin(angle)) / np.sqrt(N)
+    high = basis.astype(jnp.bfloat16)
+    low = (basis - high.astype(np.float64)).astype(jnp.bfloat16).astype(np.float64)
+    leak = (high.astype(np.float64) + low)[1:].sum(axis=1)
+    low[1:, 0] -= leak
+    low[0, 1:] -= leak
+    low = low.astype(jnp.bfloat16)
     order = (4 * np.arange(32)[None, :] + np.arange(4)[:, None]).reshape(-1)
     parts = []
-    for table in (basis, basis[:, order], basis[order, :]):
-        high = table.astype(jnp.bfloat16)
-        low = (table - high.astype(np.float64)).astype(jnp.bfloat16)
-        parts += [high, low]
+    for index in ((slice(None), slice(None)), (slice(None), order), (order, slice(None))):
+        parts += [high[index], low[index]]
     return jnp.asarray(np.stack(parts))
 
 
@@ -47,10 +51,13 @@
 
 
 def product(left, right, dims):
+    (k_left,), (k_right,) = dims
+    deep = jnp.concatenate(left, axis=k_left)
+    tall = jnp.concatenate([right[0], right[0]], axis=k_right)
     dot = functools.partial(
         lax.dot_general, dimension_numbers=(dims, ((), ())), preferred_element_type=f32
     )
-    return dot(left[0], right[0]) + (dot(left[0], right[1]) + dot(left[1], right[0]))
+    return dot(deep, tall) + dot(left[0], right[1])
 
 
 def partner_ids(x, y, c, z):
@@ -295,7 +302,7 @@
     def unheard(o):
         return o[2][0] == 2 and o[2][1] == 2
 
-    hist_order = sorted(others, key=lambda o: (unheard(o), o[2][3] > 0))
+    hist_order = sorted(others[::-1], key=unheard)
     ends = np.cumsum((0,) + STAGES)
     def hist_stage(h):
         if h == 0:

time: 38 us -> 37.2 us (0.979)
  Pallas kernels: 36 us -> 35.2 us
    pallas_call x1, Pallas kernels: 36 us -> 35.2 us  [local(): pl.pallas_call(kernel, out_shape=[pltpu.VMEM(square, f32)] * 2, in_specs=...]
where the time goes in v4:
time: 37.2 us; the launch traced here: 37.1 us
  Pallas kernels  35.2 us (95%)
  local copies, waits for them, and re-layouts  1.26 us (3%)
  between operations  0.64 us (2%)
    pallas_call x1, Pallas kernels, local(): pl.pallas_call(kernel, out_shape=[pltpu.VMEM(square, f32)] * 2, in_specs=...  35.2 us
    unnamed x2, local copies, waits for them, and re-layouts  1.26 us

profile of v4, /device:TPU:1, one launch (start us, length us, event | category | flops | bytes accessed | tf_op | source)
XLA Modules:
  0.0 37.1 jit_solution(11675515311513135598)
XLA Ops:
  0.6 35.2 %shard_map.77 = (f32[128,128]{1,0:T(8,128)S(1)}, f32[128,128]{1,0:T(8,128)S(1)}) custom-call(bf16[8,32,4,32,128]{4,3,2,1,0:T(8,128)(2,1)} %bitcast.8, f32[8]{0:T(128)} %occ_h.1, f32[128,128]{1,0:T(8,128)} %bitcast.11, f32[7,128,128]{2,1,0:T(8,128)} %bitcast.9, f32[7,128,128]{2,1,0:T(8,128)} %bitcast.10, bf16[6,128,128]{2,1,0:T(8,128)(2,1)} %constant.2.clone.tab_h), custom_call_target="tpu_custom_call" | custom-call | tf_op jit(solution)/shard_map/pallas_call | solution.py:433
  35.8 0.6 %copy.10 = f32[4,32,128]{2,1,0:T(8,128)} copy(f32[4,32,128]{2,1,0:T(8,128)S(1)} %bitcast.7) | data formatting | bytes 131072
  36.5 0.6 %copy.11 = f32[4,32,128]{2,1,0:T(8,128)} copy(f32[4,32,128]{2,1,0:T(8,128)S(1)} %bitcast.6) | data formatting | bytes 131072

commit v5 on v4

--- a/solution.py
+++ b/solution.py
@@ -426,6 +426,16 @@
     sent(vsend, 1, 2)
 
 
+def write_out(rho, v, rho_out, v_out, sem):
+    copies = [
+        pltpu.make_async_copy(rho, rho_out, sem.at[0]), pltpu.make_async_copy(v, v_out, sem.at[1])
+    ]
+    for copy in copies:
+        copy.start()
+    for copy in copies:
+        copy.wait()
+
+
 def local(orbitals, occupations, rho_in, hist_in, hist_res):
     anywhere = pl.BlockSpec(memory_space=pl.ANY)
     vmem, dma = pltpu.VMEM, pltpu.SemaphoreType.DMA
@@ -451,6 +461,14 @@
         orbitals.reshape(8, 32, 4, 32, N), occupations, rho_in.reshape(square),
         hist_in.reshape(HIST, N, N), hist_res.reshape(HIST, N, N), tables(),
     )
+    rho, v = pl.pallas_call(
+        write_out,
+        out_shape=[pltpu.HBM(square, f32)] * 2,
+        in_specs=[pl.BlockSpec(memory_space=pltpu.VMEM)] * 2,
+        out_specs=[anywhere] * 2,
+        scratch_shapes=[dma((2,))],
+        compiler_params=pltpu.CompilerParams(vmem_limit_bytes=2**20),
+    )(rho, v)
     return rho.reshape(rho_in.shape), v.reshape(rho_in.shape)
 
 

time: 37.2 us -> 36.6 us (0.984)
  local copies, waits for them, and re-layouts: 1.26 us -> 0 us
  Pallas kernels: 35.2 us -> 35.9 us
    unnamed x2 -> x0, local copies, waits for them, and re-layouts: 1.26 us -> none
    pallas_call x0 -> x1, Pallas kernels: none -> 0.67 us  [local(): pl.pallas_call(write_out, out_shape=[pltpu.HBM(square, f32)] * 2, in_spec...]
where the time goes in v5:
time: 36.6 us; the launch traced here: 36.5 us
  Pallas kernels  35.9 us (98%)
  between operations  0.64 us (2%)
    pallas_call x1, Pallas kernels, local(): pl.pallas_call(kernel, out_shape=[pltpu.VMEM(square, f32)] * 2, in_specs=...  35.2 us

profile of v5, /device:TPU:1, one launch (start us, length us, event | category | flops | bytes accessed | tf_op | source)
XLA Modules:
  0.0 36.5 jit_solution(4189096580430286268)
XLA Ops:
  0.6 35.2 %shard_map.77 = (f32[128,128]{1,0:T(8,128)S(1)}, f32[128,128]{1,0:T(8,128)S(1)}) custom-call(bf16[8,32,4,32,128]{4,3,2,1,0:T(8,128)(2,1)} %bitcast.6, f32[8]{0:T(128)} %occ_h.1, f32[128,128]{1,0:T(8,128)} %bitcast.9, f32[7,128,128]{2,1,0:T(8,128)} %bitcast.7, f32[7,128,128]{2,1,0:T(8,128)} %bitcast.8, bf16[6,128,128]{2,1,0:T(8,128)(2,1)} %constant.2.clone.tab_h), custom_call_target="tpu_custom_call" | custom-call | tf_op jit(solution)/shard_map/pallas_call | solution.py:443
  35.8 0.7 %shard_map.78 = (f32[128,128]{1,0:T(8,128)}, f32[128,128]{1,0:T(8,128)}) custom-call(f32[128,128]{1,0:T(8,128)S(1)} %get-tuple-element.6.rho, f32[128,128]{1,0:T(8,128)S(1)} %get-tuple-element.7.v), custom_call_target="tpu_custom_call" | custom-call | tf_op jit(solution)/shard_map/pallas_call | solution.py:464
